TPU v7x, 32 devices: a whole 2x2x4 slice. The times are simulated.
32 devices in a mesh: slab: 16 (over z, y, x), feat: 2 (over core).
Axes of the slice: x: 2, y: 2, z: 4, core: 2. Of those that a mesh axis runs over, the one named last changes fastest.
Arguments:
- states: float32 [40, 8192], P(None, ('slab', 'feat')), may hold values from -6 to 6
- inputs: float32 [8192], P(('slab', 'feat')), may hold values from -4 to 4
- targets: float32 [40, 8192], P(None, ('slab', 'feat')), may hold values from -4 to 4
Outputs:
- local_operators: float32 [16, 40, 862], P('slab', 'feat')
- scaled_duals: float32 [16, 40, 862], P('slab', 'feat')
- consensus: float32 [40, 862], P('feat')
- residual_history: float32 [2, 2], replicated
All inputs are finite; a program needn't handle non-finite values.
Results may differ from a plain program's by a relative error of at most 0.0003.
Values sent between devices are 32-bit elements; how exact they have to be, the bound alone decides.
No kernel may reach another device: no remote copies, remote signals or barrier semaphores. Data moves between devices by JAX's collectives and lax.ppermute only.
A program may use at most 64 MiB of HBM per device.

v0:
```python
import jax
import jax.numpy as jnp
from jax import lax
from jax.sharding import PartitionSpec as P

ITERS = 2


penalty = 1.0


def features(states, inputs):
    reduced = states.shape[0]
    blocks = [states]
    for column in range(reduced):
        blocks.append(states[column : column + 1] * states[column:])
    blocks.append(inputs[None, :])
    blocks.append(jnp.ones_like(inputs)[None, :])
    return jnp.concatenate(blocks, 0)


def product(left, right):
    return jnp.dot(left, right, precision=lax.Precision.HIGHEST, preferred_element_type=jnp.float32)


def solve_rows(factor, right_side):
    return jax.scipy.linalg.cho_solve((factor, True), right_side.T).T


def slab_average(summand):
    return lax.psum(summand, "slab")


def shards(states, inputs, targets):
    reduced = states.shape[0]
    feat_count = lax.axis_size("feat")
    slab_count = lax.axis_size("slab")
    half_rows = reduced // feat_count
    all_states, all_targets, all_inputs = (
        lax.all_gather(states, "feat", axis=1, tiled=True),
        lax.all_gather(targets, "feat", axis=1, tiled=True),
        lax.all_gather(inputs, "feat", axis=0, tiled=True),
    )
    design = features(all_states, all_inputs)
    row_total = design.shape[1]
    gram_matrix = product(design, design.T) / row_total
    first_row = lax.axis_index("feat") * half_rows
    picked = lax.dynamic_slice_in_dim(all_targets, first_row, half_rows, 0)
    cross = product(picked, design.T) / row_total
    width = gram_matrix.shape[0]
    factor = jnp.linalg.cholesky(gram_matrix + penalty * jnp.eye(width, dtype=jnp.float32))
    consensus = jnp.zeros((half_rows, width), jnp.float32)
    duals = jnp.zeros((half_rows, width), jnp.float32)
    operator_rows = duals
    primal_list = []
    dual_list = []
    for sweep in range(ITERS):
        operator_rows = solve_rows(factor, cross + penalty * (consensus - duals))
        updated = slab_average(operator_rows + duals) / slab_count
        duals = duals + operator_rows - updated
        primal_part = jnp.sum(jnp.square(operator_rows - updated))
        dual_part = penalty * penalty * jnp.sum(jnp.square(updated - consensus))
        primal_sum, dual_sum = lax.psum((primal_part, dual_part), ("slab", "feat"))
        primal_list.append(primal_sum)
        dual_list.append(dual_sum)
        consensus = updated
    history = jnp.stack([jnp.stack(primal_list), jnp.stack(dual_list)])
    residual_history = jnp.sqrt(history / (slab_count * reduced * width))
    return (operator_rows[None], duals[None], consensus, residual_history)


def solution(mesh):
    in_specs = (P(None, ("slab", "feat")), P(("slab", "feat")), P(None, ("slab", "feat")))
    out_specs = (P("slab", "feat", None), P("slab", "feat", None), P("feat", None), P())
    return jax.shard_map(shards, mesh=mesh, in_specs=in_specs, out_specs=out_specs, check_vma=False)
```

profile of v0, /device:TPU:0, one launch (start us, length us, event | category | flops | bytes accessed | tf_op | source)
XLA Modules:
  0.0 593.1 jit_solution(18076487294671778881)
XLA Ops:
  22.9 11.9 %concatenate.45 = f32[862,512]{1,0:T(8,128)S(1)} concatenate(f32[40,512]{1,0:T(8,128)S(1)} %all_gather.9, f32[40,512]{1,0:T(8,128)S(1)} %broadcast_multiply_fusion.1, f32[39,512]{1,0:T(8,128)S(1)} %slice_multiply_fusion.6, f32[38,512]{1,0:T(8,128)S(1)} %slice_multiply_fusion.5, f32[37,512]{1,0:T(8,128)S(1)} %slice_multiply_fusion.4, f32[36,512]{1,0:T(8,128)S(1)} %slice_multiply_fusion.3, ...), dimensions={0} | concatenate | bytes 3530752 | tf_op jit(solution)/shard_map/concatenate | solution.py:19
  34.8 7.8 %convert_add_fusion = (f32[862,862]{0,1:T(8,128)}, f32[862,862]{0,1:T(8,128)}) fusion(f32[862,512]{1,0:T(8,128)S(1)} %concatenate.45), kind=kOutput, calls=%fused_computation.8 | convolution fusion | flops 4568234496 | bytes 7709728 | tf_op jit(solution)/shard_map/dot_general | solution.py:23
  42.6 3.6 copy.12
  50.2 11.7 %cholesky.196 = f32[128,128]{1,0:T(8,128)S(1)} custom-call(f32[128,128]{1,0:T(8,128)S(1)} %cholesky.508), custom_call_target="Cholesky" | custom-call | tf_op jit(solution)/shard_map/jit(cholesky)/cholesky | solution.py:51
  62.1 9.8 %custom-call.56 = f32[1,128,128]{1,2,0:T(8,128)S(1)} custom-call(f32[1,128,128]{2,1,0:T(8,128)S(1)} %get-tuple-element.104), custom_call_target="InvertDiagBlocksLowerTriangular" | custom-call | tf_op jit(solution)/shard_map/jit(cholesky)/cholesky | solution.py:51
  75.5 12.5 %cholesky.217 = f32[128,128]{1,0:T(8,128)S(1)} custom-call(f32[128,128]{1,0:T(8,128)} %cholesky.512), custom_call_target="Cholesky" | custom-call | tf_op jit(solution)/shard_map/jit(cholesky)/cholesky | solution.py:51
  88.7 11.0 %custom-call.57 = f32[1,128,128]{1,2,0:T(8,128)S(1)} custom-call(f32[1,128,128]{2,1,0:T(8,128)} %get-tuple-element.101), custom_call_target="InvertDiagBlocksLowerTriangular" | custom-call | tf_op jit(solution)/shard_map/jit(cholesky)/cholesky | solution.py:51
  101.8 11.7 %cholesky.413 = f32[128,128]{1,0:T(8,128)S(1)} custom-call(f32[128,128]{1,0:T(8,128)S(1)} %cholesky.517), custom_call_target="Cholesky" | custom-call | tf_op jit(solution)/shard_map/jit(cholesky)/cholesky | solution.py:51
  113.5 9.8 %custom-call.58 = f32[1,128,128]{1,2,0:T(8,128)S(1)} custom-call(f32[1,128,128]{2,1,0:T(8,128)S(1)} %get-tuple-element.98), custom_call_target="InvertDiagBlocksLowerTriangular" | custom-call | tf_op jit(solution)/shard_map/jit(cholesky)/cholesky | solution.py:51
  125.4 11.9 %cholesky.432 = f32[128,128]{1,0:T(8,128)S(1)} custom-call(f32[128,128]{1,0:T(8,128)S(1)} %cholesky.522), custom_call_target="Cholesky" | custom-call | tf_op jit(solution)/shard_map/jit(cholesky)/cholesky | solution.py:51
  137.3 9.8 %custom-call.59 = f32[1,128,128]{1,2,0:T(8,128)S(1)} custom-call(f32[1,128,128]{2,1,0:T(8,128)S(1)} %get-tuple-element.95), custom_call_target="InvertDiagBlocksLowerTriangular" | custom-call | tf_op jit(solution)/shard_map/jit(cholesky)/cholesky | solution.py:51
  149.1 11.7 %cholesky.451 = f32[128,128]{1,0:T(8,128)S(1)} custom-call(f32[128,128]{1,0:T(8,128)S(1)} %cholesky.527), custom_call_target="Cholesky" | custom-call | tf_op jit(solution)/shard_map/jit(cholesky)/cholesky | solution.py:51
  160.9 9.8 %custom-call.60 = f32[1,128,128]{1,2,0:T(8,128)S(1)} custom-call(f32[1,128,128]{2,1,0:T(8,128)S(1)} %get-tuple-element.92), custom_call_target="InvertDiagBlocksLowerTriangular" | custom-call | tf_op jit(solution)/shard_map/jit(cholesky)/cholesky | solution.py:51
  172.5 11.9 %cholesky.471 = f32[128,128]{1,0:T(8,128)S(1)} custom-call(f32[128,128]{1,0:T(8,128)S(1)} %cholesky.532), custom_call_target="Cholesky" | custom-call | tf_op jit(solution)/shard_map/jit(cholesky)/cholesky | solution.py:51
  184.4 9.8 %custom-call.61 = f32[1,128,128]{1,2,0:T(8,128)S(1)} custom-call(f32[1,128,128]{2,1,0:T(8,128)S(1)} %get-tuple-element.89), custom_call_target="InvertDiagBlocksLowerTriangular" | custom-call | tf_op jit(solution)/shard_map/jit(cholesky)/cholesky | solution.py:51
  195.6 8.6 %cholesky.492 = f32[94,94]{1,0:T(8,128)S(1)} custom-call(f32[94,94]{1,0:T(8,128)S(1)} %convolution_subtract_fusion.5), custom_call_target="Cholesky" | custom-call | tf_op jit(solution)/shard_map/jit(cholesky)/cholesky | solution.py:51
  214.6 17.4 %while.4 = (s32[]{:T(128)}, f32[862,862]{1,0:T(8,128)}, s32[6,2]{0,1:T(2,128)S(1)}, f32[6,128,128]{2,1,0:T(8,128)S(1)}, s32[]{:T(128)}) while((s32[]{:T(128)}, f32[862,862]{1,0:T(8,128)}, s32[6,2]{0,1:T(2,128)S(1)}, f32[6,128,128]{2,1,0:T(8,128)S(1)}, s32[]{:T(128)}) %tuple.120), condition=%wide.while_cond.clone, body=%wide.while_body.clone.sunk | while | flops 2 | bytes 131189 | solution.py:27
  215.2 2.3 bitcast_dynamic-update-slice_fusion.2
  218.1 2.3 bitcast_dynamic-update-slice_fusion.2
  234.0 69.8 %custom-call.64 = f32[7,128,128]{1,2,0:T(8,128)S(1)} custom-call(f32[7,128,128]{2,1,0:T(8,128)} %pad_maximum_fusion), custom_call_target="InvertDiagBlocksLowerTriangular" | custom-call | tf_op jit(solution)/shard_map/jit(_cho_solve)/triangular_solve | solution.py:27
  303.8 3.1 convolution_multiply_fusion
  317.7 107.1 %all-reduce.7.cloned.1.call-done = f32[20,862]{1,0:T(8,128)} async-done(((f32[20,862]{1,0:T(8,128)}), f32[20,862]{1,0:T(8,128)}) %all-reduce.7.cloned.1.call-update) | async-done | bytes 68976 | tf_op jit(solution)/shard_map/psum | solution.py:31
  434.7 103.8 %all-reduce.9.cloned.1.call-done = f32[20,862]{1,0:T(8,128)} async-done(((f32[20,862]{1,0:T(8,128)}), f32[20,862]{1,0:T(8,128)}) %all-reduce.9.cloned.1.call-update) | async-done | bytes 68976 | tf_op jit(solution)/shard_map/psum | solution.py:31
  541.9 40.7 %all-reduce.3 = (f32[1]{0:T(128)}, f32[1]{0:T(128)}, f32[1]{0:T(128)}, f32[1]{0:T(128)}) all-reduce(f32[1]{0:T(128)} %bitcast.80, f32[1]{0:T(128)} %bitcast.79, f32[1]{0:T(128)} %bitcast.77, f32[1]{0:T(128)} %bitcast.76), channel_id=1, replica_groups=mesh['slab'=16,'feat'=2] {'slab','feat'}, use_global_device_ids=true, to_apply=%region_23.25 | all-reduce | flops 4 | bytes 32 | tf_op jit(solution)/shard_map/psum | solution.py:63
  (223 shorter events, 80.4 us)
Async XLA Ops:
  7.2 11.2 %copy-start.10 = (f32[256]{0:T(256)S(1)}, f32[256]{0:T(256)}, u32[]{:S(2)}) copy-start(f32[256]{0:T(256)} %param.6) | copy-start | bytes 3076
  7.2 13.2 %copy-start.8 = (f32[40,256]{1,0:T(8,128)S(1)}, f32[40,256]{1,0:T(8,128)}, u32[]{:S(2)}) copy-start(f32[40,256]{1,0:T(8,128)} %param.7) | copy-start | bytes 122884
  7.2 417.6 %all-reduce.7.cloned.1.call-start = ((), (), s32[]{:S(2)}) async-start(), calls=%async_computation | async-start | bytes 172032 | tf_op jit(solution)/shard_map/psum | solution.py:31
  34.8 7.8 %copy-start = (f32[862,512]{1,0:T(8,128)}, f32[862,512]{1,0:T(8,128)S(1)}, u32[]{:S(2)}) copy-start(f32[862,512]{1,0:T(8,128)S(1)} %concatenate.45) | copy-start | bytes 5296132
  48.5 1.6 copy-start.3
  212.7 0.9 copy-start.9
  212.7 0.9 copy-start.11
  212.7 1.9 copy-start.6
  213.0 1.7 copy-start.1
  232.1 75.0 %copy-start.2 = (f32[862,862]{1,0:T(8,128)S(1)}, f32[862,862]{1,0:T(8,128)}, u32[]{:S(2)}) copy-start(f32[862,862]{1,0:T(8,128)} %get-tuple-element.201) | copy-start | bytes 8916532
  306.9 10.8 %copy-start.4 = (f32[20,862]{1,0:T(8,128)}, f32[20,862]{1,0:T(8,128)S(1)}, u32[]{:S(2)}) copy-start(f32[20,862]{1,0:T(8,128)S(1)} %convolution_multiply_fusion) | copy-start | bytes 206884
  317.7 220.9 %all-reduce.9.cloned.1.call-start = ((), (), s32[]{:S(2)}) async-start(), calls=%async_computation.1 | async-start | bytes 172032 | tf_op jit(solution)/shard_map/psum | solution.py:31
  424.8 7.6 %copy-start.5 = (f32[20,862]{1,0:T(8,128)S(1)}, f32[20,862]{1,0:T(8,128)}, u32[]{:S(2)}) copy-start(f32[20,862]{1,0:T(8,128)} %all-reduce.7.cloned.1.call-done) | copy-start | bytes 206884
  540.3 45.6 %copy-start.7 = (f32[20,862]{1,0:T(8,128)}, f32[20,862]{1,0:T(8,128)S(1)}, u32[]{:S(2)}) copy-start(f32[20,862]{1,0:T(8,128)S(1)} %get-tuple-element.45) | copy-start | bytes 206884
Sparse Core Ops, SparseCore 0:
  317.8 106.9 all-reduce.6
  434.1 104.3 all-reduce.8
where the time goes:
time: 600 us; the launch traced here: 593 us
  other arithmetic  236 us (39%)
  waiting for transfers between devices  211 us (35%)
  blocking collectives  46.8 us (8%)
  local copies, waits for them, and re-layouts  42.8 us (7%)
  matrix products  36.1 us (6%)
  between operations  20.1 us (3%)
    psum x2, waiting for transfers between devices, slab_average(): return lax.psum(summand, 'slab')  211 us
    another operation x26, other arithmetic, shards(): jnp.linalg.cholesky(gram_matrix + penalty * jnp.eye(width, dtype=jnp.floa...  145 us
    another operation x8, other arithmetic, solve_rows(): return jax.scipy.linalg.cho_solve((factor, True), right_side.T).T  73 us
    psum x1, blocking collectives, shards(): primal_sum, dual_sum = lax.psum((primal_part, dual_part), ('slab', 'feat'))  40.7 us
    another operation x26, local copies, waits for them, and re-layouts, solve_rows(): return jax.scipy.linalg.cho_solve((factor, True), right_side.T).T  18.6 us
    another operation x52, matrix products, solve_rows(): return jax.scipy.linalg.cho_solve((factor, True), right_side.T).T  13.1 us
    another operation x12, matrix products, shards(): jnp.linalg.cholesky(gram_matrix + penalty * jnp.eye(width, dtype=jnp.floa...  12.1 us
  transfers between devices with their start and end apart: 2, of which 2 were waited for; matrix products, arithmetic and copies ran while one was open for 0% of the time, Pallas kernels for 0%

commit v1 on v0

v1 whole, which is shorter than its diff:
```python
import jax
import jax.numpy as jnp
from jax import lax
from jax.experimental import pallas as pl
from jax.experimental.pallas import tpu as pltpu
from jax.sharding import PartitionSpec as P

penalty = 1.0
F32 = jnp.float32
BF16 = jnp.bfloat16
NN = (((1,), (0,)), ((), ()))
NT = (((1,), (1,)), ((), ()))
TN = (((0,), (0,)), ((), ()))


def mxu(left, right, dims):
    return lax.dot_general(left, right, dims, preferred_element_type=F32)


def split(value):
    high = value.astype(BF16)
    return high, (value - high.astype(F32)).astype(BF16)


def product3(left, right, dims):
    left_high, left_low = left
    right_high, right_low = right
    return mxu(left_high, right_high, dims) + (mxu(left_high, right_low, dims) + mxu(left_low, right_high, dims))


def product(left, right, dims):
    return lax.dot_general(left, right, dims, precision=lax.Precision.HIGHEST, preferred_element_type=F32)


def unit(size):
    return (lax.broadcasted_iota(jnp.int32, (size, size), 0) == lax.broadcasted_iota(jnp.int32, (size, size), 1)).astype(F32)


def refined(right_side, high, low, inverse, rounds):
    inverse_high, inverse_low = inverse
    answer = product3(split(right_side), inverse, NN)
    for _ in range(rounds):
        gap = right_side - product3(split(answer), (high, low), NN)
        answer = answer + mxu(gap.astype(BF16), inverse_high, NN)
    return answer


def first_kernel(states, inputs, targets, operator, phi_high, phi_low, kernel_high, kernel_low, inverse_high, inverse_low, phi, inverse):
    reduced, rows = states.shape
    x = states[...]
    u = inputs[...]
    width = phi.shape[0]
    offset = 0
    phi[0:reduced, :] = x
    offset = reduced
    for column in range(reduced):
        count = reduced - column
        phi[offset : offset + count, :] = x[column : column + 1] * x[column:]
        offset += count
    phi[offset : offset + 1, :] = u
    phi[offset + 1 : offset + 2, :] = jnp.ones_like(u)
    phi[offset + 2 :, :] = jnp.zeros((width - offset - 2, rows), F32)
    whole = phi[...]
    phi_high[...] = whole.astype(BF16)
    phi_low[...] = (whole - whole.astype(BF16).astype(F32)).astype(BF16)
    scale = 1.0 / (rows * penalty)
    inner = product(x, x, TN)
    squares = product(x * x, x * x, TN)
    ends = jnp.concatenate([u, jnp.ones_like(u), jnp.zeros((6, rows), F32)], 0)
    system = inner + 0.5 * (inner * inner + squares) + product(ends, ends, TN)
    identity = unit(rows)
    system = system * scale + identity
    bound = jnp.max(jnp.sum(jnp.abs(system), axis=0))
    high = system.astype(BF16)
    kernel_high[...] = high
    kernel_low[...] = (system - high.astype(F32)).astype(BF16)
    mu = 2.0 / (1.0 + bound)
    delta = (bound - 1.0) / (bound + 1.0)
    inverse[...] = mu * (2.0 * identity - mu * system)
    low_end = 1.0 - delta * delta

    def coarse_more(carry):
        step, low_end = carry
        return jnp.logical_and(low_end < 0.9, step < 40)

    def coarse(carry):
        step, low_end = carry
        s = 2.0 / (1.0 + low_end)
        guess = inverse[...]
        guess_high = guess.astype(BF16)
        gap = unit(rows) - s * mxu(kernel_high[...], guess_high, NN)
        inverse[...] = s * (guess + mxu(guess_high, gap.astype(BF16), NN))
        shrink = (1.0 - low_end) / (1.0 + low_end)
        return step + 1, 1.0 - shrink * shrink

    lax.while_loop(coarse_more, coarse, (jnp.int32(0), low_end))

    def residual():
        return unit(rows) - product3((kernel_high[...], kernel_low[...]), split(inverse[...]), NN)

    start_gap = residual()
    start = jnp.sum(start_gap * start_gap)
    bad = jnp.logical_not(start < 0.5)

    @pl.when(bad)
    def _():
        inverse[...] = mu * unit(rows)

    @pl.when(jnp.logical_not(bad))
    def _():
        guess = inverse[...]
        inverse[...] = guess + product3(split(guess), split(start_gap), NN)

    def fine_more(carry):
        step, size = carry
        return jnp.logical_and(size > 1e-3, step < 60)

    def fine(carry):
        step, _ = carry
        gap = residual()
        guess = inverse[...]
        inverse[...] = guess + product3(split(guess), split(gap), NN)
        return step + 1, jnp.sum(gap * gap)

    lax.while_loop(fine_more, fine, (jnp.int32(0), jnp.where(bad, 1.0, start)))
    found_high, found_low = split(inverse[...])
    inverse_high[...] = found_high
    inverse_low[...] = found_low
    answer = refined(targets[...] * scale, kernel_high[...], kernel_low[...], (found_high, found_low), 1)
    operator[...] = product3(split(answer), (phi_high[...], phi_low[...]), NT)


def second_kernel(slabs, features, half_rows, targets, operator, total, phi_high, phi_low, kernel_high, kernel_low, inverse_high, inverse_low, mean_out, next_operator, summand):
    rows = targets.shape[1]
    scale = 1.0 / (rows * penalty)
    first = operator[...]
    mean = total[...] / slabs
    duals = first - mean
    shifted = mean - duals
    phi = (phi_high[...], phi_low[...])
    kernel = (kernel_high[...], kernel_low[...])
    right_side = (targets[...] - product3(split(shifted), phi, NN)) * scale
    answer = refined(right_side, kernel[0], kernel[1], (inverse_high[...], inverse_low[...]), 1)
    second = shifted + product3(split(answer), phi, NT)
    mean_out[...] = mean
    next_operator[...] = second
    primal = jnp.sum(duals * duals)
    moved = second - mean
    spread = jnp.sum(moved * moved)
    row = lax.broadcasted_iota(jnp.int32, first.shape, 0)
    column = lax.broadcasted_iota(jnp.int32, first.shape, 1)
    extra = jnp.where(column == 0, primal, jnp.where(column == 1, spread, 0.0))
    summand[...] = jnp.where(row == half_rows, extra, second + duals)


def slab_sum(value, slab_count):
    step = 1
    while step < slab_count:
        pairs = [(i, i ^ step) for i in range(slab_count)]
        value = value + lax.ppermute(value, "slab", pairs)
        step *= 2
    return value


def shards(states, inputs, targets):
    reduced, part = states.shape
    feat_count = lax.axis_size("feat")
    slab_count = lax.axis_size("slab")
    half_rows = reduced // feat_count
    rows = part * feat_count
    features = reduced + reduced * (reduced + 1) // 2 + 2
    width = (features + 127) // 128 * 128
    height = (half_rows // 8 + 1) * 8
    core = lax.axis_index("feat")
    swap = [(i, (i + 1) % feat_count) for i in range(feat_count)]
    own = lax.dynamic_slice_in_dim(targets, core * half_rows, half_rows, 0)
    theirs = lax.dynamic_slice_in_dim(targets, (1 - core) * half_rows, half_rows, 0)
    packed = jnp.concatenate([states, theirs, inputs[None]], 0)
    other = lax.ppermute(packed, "feat", swap)
    all_states = jnp.concatenate([states, other[:reduced]], 1)
    all_inputs = jnp.concatenate([inputs[None], other[reduced + half_rows :]], 1)
    picked = jnp.concatenate([own, other[reduced : reduced + half_rows]], 1)
    picked = jnp.pad(picked, ((0, height - half_rows), (0, 0)))
    shape = jax.ShapeDtypeStruct
    flat = shape((height, width), F32)
    operator, *kept = pl.pallas_call(
        first_kernel,
        out_shape=(flat, shape((width, rows), BF16), shape((width, rows), BF16)) + (shape((rows, rows), BF16),) * 4,
        scratch_shapes=[pltpu.VMEM((width, rows), F32), pltpu.VMEM((rows, rows), F32)],
        name="first_solve",
    )(all_states, all_inputs, picked)
    total = slab_sum(operator, slab_count)

    def second(*refs):
        second_kernel(slab_count, features, half_rows, *refs)

    mean, second_operator, summand = pl.pallas_call(second, out_shape=(flat, flat, flat), name="second_solve")(
        picked, operator, total, *kept
    )
    total = slab_sum(summand, slab_count)
    keep = lambda value: value[:half_rows, :features]
    consensus = keep(total) / slab_count
    before = keep(mean)
    duals = keep(operator) - before + keep(second_operator) - consensus
    first_dual = slab_count * penalty * penalty * jnp.sum(jnp.square(before))
    moved = slab_count * jnp.sum(jnp.square(consensus - before))
    sums = jnp.stack([total[half_rows, 0], total[half_rows, 1] - moved, first_dual, penalty * penalty * moved])
    sums = sums + lax.ppermute(sums, "feat", swap)
    history = jnp.maximum(sums, 0.0).reshape(2, 2)
    residual_history = jnp.sqrt(history / (slab_count * reduced * features))
    return (keep(second_operator)[None], duals[None], consensus, residual_history)


def solution(mesh):
    in_specs = (P(None, ("slab", "feat")), P(("slab", "feat")), P(None, ("slab", "feat")))
    out_specs = (P("slab", "feat", None), P("slab", "feat", None), P("feat", None), P())
    return jax.shard_map(shards, mesh=mesh, in_specs=in_specs, out_specs=out_specs, check_vma=False)
```

time: 600 us -> 91 us (0.15)
  other arithmetic: 236 us -> 6.46 us
  waiting for transfers between devices: 211 us -> 23.6 us
  blocking collectives: 46.8 us -> 0 us
  local copies, waits for them, and re-layouts: 42.8 us -> 4.17 us
  matrix products: 36.1 us -> 0 us
  starting transfers between devices: 0.08 us -> 33.4 us
  Pallas kernels: 0 us -> 19.6 us
  between operations: 20.1 us -> 2.68 us
    another operation x36 -> x1, other arithmetic: 221 us -> 0.71 us  [shards(): jnp.stack([total[half_rows, 0], total[half_rows, 1] - moved, first_dual,...]
    psum x2 -> x0, waiting for transfers between devices: 211 us -> none  [slab_average(): return lax.psum(summand, 'slab')]
    psum x1 -> x0, blocking collectives: 40.7 us -> none  [shards(): primal_sum, dual_sum = lax.psum((primal_part, dual_part), ('slab', 'feat'))]
    ppermute x0 -> x10, starting transfers between devices: none -> 33.4 us  [the longest x8 32.8 us: slab_sum(): value = value + lax.ppermute(value, 'slab', pairs)]
    another operation x64 -> x0, matrix products: 25.2 us -> none  [the longest x52 13.1 us: solve_rows(): return jax.scipy.linalg.cho_solve((factor, True), right_side.T).T]
    ppermute x0 -> x10, waiting for transfers between devices: none -> 23.6 us  [the longest x8 22.3 us: slab_sum(): value = value + lax.ppermute(value, 'slab', pairs)]
    another operation x34 -> x0, local copies, waits for them, and re-layouts: 20.1 us -> none  [the longest x26 18.6 us: solve_rows(): return jax.scipy.linalg.cho_solve((factor, True), right_side.T).T]
    pallas_call x0 -> x2, Pallas kernels: none -> 19.6 us  [the longest x1 14.5 us: shards(): pl.pallas_call(first_kernel, out_shape=(flat, shape((width, rows), BF16),...]
  transfers between devices with their start and end apart: 2 -> 10, of which waited for: 2 -> 10; matrix products, arithmetic and copies ran while one was open for 0% -> 1% of each run, Pallas kernels for 0% -> 0%
where the time goes in v1:
time: 91 us; the launch traced here: 90 us
  starting transfers between devices  33.4 us (37%)
  waiting for transfers between devices  23.6 us (26%)
  Pallas kernels  19.6 us (22%)
  other arithmetic  6.46 us (7%)
  local copies, waits for them, and re-layouts  4.17 us (5%)
  between operations  2.68 us (3%)
    ppermute x8, starting transfers between devices, slab_sum(): value = value + lax.ppermute(value, 'slab', pairs)  32.8 us
    ppermute x8, waiting for transfers between devices, slab_sum(): value = value + lax.ppermute(value, 'slab', pairs)  22.3 us
    pallas_call x1, Pallas kernels, shards(): pl.pallas_call(first_kernel, out_shape=(flat, shape((width, rows), BF16),...  14.5 us
    pallas_call x1, Pallas kernels, shards(): pl.pallas_call(second, out_shape=(flat, flat, flat), name='second_solve')  5.15 us
    add x8, other arithmetic, slab_sum(): value = value + lax.ppermute(value, 'slab', pairs)  2.51 us
    unnamed x14, local copies, waits for them, and re-layouts  2.1 us
  transfers between devices with their start and end apart: 10, of which 10 were waited for; matrix products, arithmetic and copies ran while one was open for 1% of the time, Pallas kernels for 0%

profile of v1, /device:TPU:0, one launch (start us, length us, event | category | flops | bytes accessed | tf_op | source)
XLA Modules:
  0.0 90.0 jit_solution(3006917034529667815)
XLA Ops:
  0.6 0.8 constant_dynamic-slice_fusion.1
  2.7 0.9 %collective-permute-done = f32[61,256]{1,0:T(8,128)S(1)} collective-permute-done((f32[61,256]{1,0:T(8,128)S(1)}, f32[61,256]{1,0:T(8,128)S(1)}, u32[]{:S(2)}, u32[]{:S(2)}) %collective-permute-start) | collective-permute-done | bytes 62496 | tf_op jit(solution)/shard_map/ppermute | solution.py:179
  5.5 14.5 %first_solve.1 = (f32[24,896]{1,0:T(8,128)}, bf16[896,512]{1,0:T(8,128)(2,1)}, bf16[896,512]{1,0:T(8,128)(2,1)}, bf16[512,512]{1,0:T(8,128)(2,1)}, bf16[512,512]...) custom-call(f32[40,512]{1,0:T(8,128)} %pad_maximum_fusion.states, ...), custom_call_target="tpu_custom_call" | custom-call | tf_op jit(solution)/shard_map/first_solve/pallas_call | solution.py:186
  20.0 2.0 %collective-permute-start.1 = (f32[24,896]{1,0:T(8,128)}, f32[24,896]{1,0:T(8,128)S(1)}, u32[]{:S(2)}, u32[]{:S(2)}) collective-permute-start(f32[24,896]{1,0:T(8,128)} %get-tuple-element.14.refs_1_), channel_id=1, source_target_pairs={{0,2},{2,0},{4,6},{6,4},{8,10},{10,8},{12,14},{14,12},{16,18},{18,... | collective-permute-start | bytes 258056 | tf_op jit(solution)/shard_map/ppermute | solution.py:160
  22.0 3.1 %collective-permute-done.1 = f32[24,896]{1,0:T(8,128)S(1)} collective-permute-done((f32[24,896]{1,0:T(8,128)}, f32[24,896]{1,0:T(8,128)S(1)}, u32[]{:S(2)}, u32[]{:S(2)}) %collective-permute-start.1) | collective-permute-done | bytes 86048 | tf_op jit(solution)/shard_map/ppermute | solution.py:160
  25.1 0.9 add.40
  26.0 2.6 %collective-permute-start.2 = (f32[24,896]{1,0:T(8,128)S(1)}, f32[24,896]{1,0:T(8,128)S(1)}, u32[]{:S(2)}, u32[]{:S(2)}) collective-permute-start(f32[24,896]{1,0:T(8,128)S(1)} %add.40), channel_id=1, source_target_pairs={{0,4},{2,6},{4,0},{6,2},{8,12},{10,14},{12,8},{14,10},{16,20},{18,... | collective-permute-start | bytes 258056 | tf_op jit(solution)/shard_map/ppermute | solution.py:160
  28.6 2.5 %collective-permute-done.2 = f32[24,896]{1,0:T(8,128)S(1)} collective-permute-done((f32[24,896]{1,0:T(8,128)S(1)}, f32[24,896]{1,0:T(8,128)S(1)}, u32[]{:S(2)}, u32[]{:S(2)}) %collective-permute-start.2) | collective-permute-done | bytes 86048 | tf_op jit(solution)/shard_map/ppermute | solution.py:160
  31.1 15.5 %collective-permute-start.3 = (f32[24,896]{1,0:T(8,128)S(1)}, f32[24,896]{1,0:T(8,128)S(1)}, u32[]{:S(2)}, u32[]{:S(2)}) collective-permute-start(f32[24,896]{1,0:T(8,128)S(1)} %add.41), channel_id=1, source_target_pairs={{0,8},{2,10},{4,12},{6,14},{8,0},{10,2},{12,4},{14,6},{16,24},{18,... | collective-permute-start | bytes 258056 | tf_op jit(solution)/shard_map/ppermute | solution.py:160
  46.6 2.5 %collective-permute-done.3 = f32[24,896]{1,0:T(8,128)S(1)} collective-permute-done((f32[24,896]{1,0:T(8,128)S(1)}, f32[24,896]{1,0:T(8,128)S(1)}, u32[]{:S(2)}, u32[]{:S(2)}) %collective-permute-start.3) | collective-permute-done | bytes 86048 | tf_op jit(solution)/shard_map/ppermute | solution.py:160
  49.1 4.8 %collective-permute-start.4 = (f32[24,896]{1,0:T(8,128)S(1)}, f32[24,896]{1,0:T(8,128)S(1)}, u32[]{:S(2)}, u32[]{:S(2)}) collective-permute-start(f32[24,896]{1,0:T(8,128)S(1)} %add.42), channel_id=1, source_target_pairs={{0,16},{2,18},{4,20},{6,22},{8,24},{10,26},{12,28},{14,30},{16,0},... | collective-permute-start | bytes 258056 | tf_op jit(solution)/shard_map/ppermute | solution.py:160
  53.9 2.5 %collective-permute-done.4 = f32[24,896]{1,0:T(8,128)S(1)} collective-permute-done((f32[24,896]{1,0:T(8,128)S(1)}, f32[24,896]{1,0:T(8,128)S(1)}, u32[]{:S(2)}, u32[]{:S(2)}) %collective-permute-start.4) | collective-permute-done | bytes 86048 | tf_op jit(solution)/shard_map/ppermute | solution.py:160
  57.0 5.2 %second_solve.1 = (f32[24,896]{1,0:T(8,128)}, f32[24,896]{1,0:T(8,128)}, f32[24,896]{1,0:T(8,128)}) custom-call(f32[24,512]{1,0:T(8,128)} %select_maximum_fusion.targets.refs_0_, f32[24,896]{1,0:T(8,128)} %get-tuple-element.14.refs_1_, f32[24,896]{1,0:T(8,128)} %add.43.refs_2_, bf16[896,512]{1,0:T(8,128)(2,1)} %get-tuple-element.15.refs_3_, ...), custom_call_target="tpu_custom_call" | custom-call | tf_op jit(solution)/shard_map/second_solve/pallas_call | solution.py:197
  62.5 4.4 %collective-permute-done.5 = f32[24,896]{1,0:T(8,128)S(1)} collective-permute-done((f32[24,896]{1,0:T(8,128)}, f32[24,896]{1,0:T(8,128)S(1)}, u32[]{:S(2)}, u32[]{:S(2)}) %collective-permute-start.5) | collective-permute-done | bytes 86048 | tf_op jit(solution)/shard_map/ppermute | solution.py:160
  66.9 0.9 %add.45 = f32[24,896]{1,0:T(8,128)S(1)} add(f32[24,896]{1,0:T(8,128)} %get-tuple-element.23, f32[24,896]{1,0:T(8,128)S(1)} %collective-permute-done.5) | non-fusion elementwise | flops 21504 | bytes 258048 | tf_op jit(solution)/shard_map/add | solution.py:160
  67.8 2.1 %collective-permute-start.6 = (f32[24,896]{1,0:T(8,128)S(1)}, f32[24,896]{1,0:T(8,128)S(1)}, u32[]{:S(2)}, u32[]{:S(2)}) collective-permute-start(f32[24,896]{1,0:T(8,128)S(1)} %add.45), channel_id=1, source_target_pairs={{0,4},{2,6},{4,0},{6,2},{8,12},{10,14},{12,8},{14,10},{16,20},{18,... | collective-permute-start | bytes 258056 | tf_op jit(solution)/shard_map/ppermute | solution.py:160
  69.9 2.5 %collective-permute-done.6 = f32[24,896]{1,0:T(8,128)S(1)} collective-permute-done((f32[24,896]{1,0:T(8,128)S(1)}, f32[24,896]{1,0:T(8,128)S(1)}, u32[]{:S(2)}, u32[]{:S(2)}) %collective-permute-start.6) | collective-permute-done | bytes 86048 | tf_op jit(solution)/shard_map/ppermute | solution.py:160
  72.4 2.0 %collective-permute-start.7 = (f32[24,896]{1,0:T(8,128)S(1)}, f32[24,896]{1,0:T(8,128)S(1)}, u32[]{:S(2)}, u32[]{:S(2)}) collective-permute-start(f32[24,896]{1,0:T(8,128)S(1)} %add.46), channel_id=1, source_target_pairs={{0,8},{2,10},{4,12},{6,14},{8,0},{10,2},{12,4},{14,6},{16,24},{18,... | collective-permute-start | bytes 258056 | tf_op jit(solution)/shard_map/ppermute | solution.py:160
  74.4 2.5 %collective-permute-done.7 = f32[24,896]{1,0:T(8,128)S(1)} collective-permute-done((f32[24,896]{1,0:T(8,128)S(1)}, f32[24,896]{1,0:T(8,128)S(1)}, u32[]{:S(2)}, u32[]{:S(2)}) %collective-permute-start.7) | collective-permute-done | bytes 86048 | tf_op jit(solution)/shard_map/ppermute | solution.py:160
  77.0 3.4 %collective-permute-start.8 = (f32[24,896]{1,0:T(8,128)S(1)}, f32[24,896]{1,0:T(8,128)S(1)}, u32[]{:S(2)}, u32[]{:S(2)}) collective-permute-start(f32[24,896]{1,0:T(8,128)S(1)} %add.47), channel_id=1, source_target_pairs={{0,16},{2,18},{4,20},{6,22},{8,24},{10,26},{12,28},{14,30},{16,0},... | collective-permute-start | bytes 258056 | tf_op jit(solution)/shard_map/ppermute | solution.py:160
  80.3 2.5 %collective-permute-done.8 = f32[24,896]{1,0:T(8,128)S(1)} collective-permute-done((f32[24,896]{1,0:T(8,128)S(1)}, f32[24,896]{1,0:T(8,128)S(1)}, u32[]{:S(2)}, u32[]{:S(2)}) %collective-permute-start.8) | collective-permute-done | bytes 86048 | tf_op jit(solution)/shard_map/ppermute | solution.py:160
  85.4 0.7 copy.8
  86.7 0.7 pad_maximum_fusion.3
  88.6 0.7 multiply_sqrt_fusion
  (34 shorter events, 7.2 us)
Async XLA Ops:
  0.6 0.9 copy-start.3
  1.5 0.7 copy-start.5
  2.2 1.5 %collective-permute-start = (f32[61,256]{1,0:T(8,128)S(1)}, f32[61,256]{1,0:T(8,128)S(1)}, u32[]{:S(2)}, u32[]{:S(2)}) collective-permute-start(f32[61,256]{1,0:T(8,128)S(1)} %pad_maximum_fusion.1), channel_id=1, source_target_pairs={{0,1},{1,0},{2,3},{3,2},{4,5},{5,4},{6,7},{7,6},{8,9},{9,8},{10,11... | collective-permute-start | bytes 187400 | tf_op jit(solution)/shard_map/ppermute | solution.py:179
  20.0 5.1 %collective-permute-start.1 = (f32[24,896]{1,0:T(8,128)}, f32[24,896]{1,0:T(8,128)S(1)}, u32[]{:S(2)}, u32[]{:S(2)}) collective-permute-start(f32[24,896]{1,0:T(8,128)} %get-tuple-element.14.refs_1_), channel_id=1, source_target_pairs={{0,2},{2,0},{4,6},{6,4},{8,10},{10,8},{12,14},{14,12},{16,18},{18,... | collective-permute-start | bytes 258056 | tf_op jit(solution)/shard_map/ppermute | solution.py:160
  26.0 5.1 %collective-permute-start.2 = (f32[24,896]{1,0:T(8,128)S(1)}, f32[24,896]{1,0:T(8,128)S(1)}, u32[]{:S(2)}, u32[]{:S(2)}) collective-permute-start(f32[24,896]{1,0:T(8,128)S(1)} %add.40), channel_id=1, source_target_pairs={{0,4},{2,6},{4,0},{6,2},{8,12},{10,14},{12,8},{14,10},{16,20},{18,... | collective-permute-start | bytes 258056 | tf_op jit(solution)/shard_map/ppermute | solution.py:160
  31.1 18.0 %collective-permute-start.3 = (f32[24,896]{1,0:T(8,128)S(1)}, f32[24,896]{1,0:T(8,128)S(1)}, u32[]{:S(2)}, u32[]{:S(2)}) collective-permute-start(f32[24,896]{1,0:T(8,128)S(1)} %add.41), channel_id=1, source_target_pairs={{0,8},{2,10},{4,12},{6,14},{8,0},{10,2},{12,4},{14,6},{16,24},{18,... | collective-permute-start | bytes 258056 | tf_op jit(solution)/shard_map/ppermute | solution.py:160
  49.1 7.3 %collective-permute-start.4 = (f32[24,896]{1,0:T(8,128)S(1)}, f32[24,896]{1,0:T(8,128)S(1)}, u32[]{:S(2)}, u32[]{:S(2)}) collective-permute-start(f32[24,896]{1,0:T(8,128)S(1)} %add.42), channel_id=1, source_target_pairs={{0,16},{2,18},{4,20},{6,22},{8,24},{10,26},{12,28},{14,30},{16,0},... | collective-permute-start | bytes 258056 | tf_op jit(solution)/shard_map/ppermute | solution.py:160
  62.2 4.7 %collective-permute-start.5 = (f32[24,896]{1,0:T(8,128)}, f32[24,896]{1,0:T(8,128)S(1)}, u32[]{:S(2)}, u32[]{:S(2)}) collective-permute-start(f32[24,896]{1,0:T(8,128)} %get-tuple-element.23), channel_id=1, source_target_pairs={{0,2},{2,0},{4,6},{6,4},{8,10},{10,8},{12,14},{14,12},{16,18},{18,... | collective-permute-start | bytes 258056 | tf_op jit(solution)/shard_map/ppermute | solution.py:160
  67.8 4.6 %collective-permute-start.6 = (f32[24,896]{1,0:T(8,128)S(1)}, f32[24,896]{1,0:T(8,128)S(1)}, u32[]{:S(2)}, u32[]{:S(2)}) collective-permute-start(f32[24,896]{1,0:T(8,128)S(1)} %add.45), channel_id=1, source_target_pairs={{0,4},{2,6},{4,0},{6,2},{8,12},{10,14},{12,8},{14,10},{16,20},{18,... | collective-permute-start | bytes 258056 | tf_op jit(solution)/shard_map/ppermute | solution.py:160
  72.4 4.6 %collective-permute-start.7 = (f32[24,896]{1,0:T(8,128)S(1)}, f32[24,896]{1,0:T(8,128)S(1)}, u32[]{:S(2)}, u32[]{:S(2)}) collective-permute-start(f32[24,896]{1,0:T(8,128)S(1)} %add.46), channel_id=1, source_target_pairs={{0,8},{2,10},{4,12},{6,14},{8,0},{10,2},{12,4},{14,6},{16,24},{18,... | collective-permute-start | bytes 258056 | tf_op jit(solution)/shard_map/ppermute | solution.py:160
  76.9 6.4 %copy-start.1 = (f32[24,896]{1,0:T(8,128)S(1)}, f32[24,896]{1,0:T(8,128)}, u32[]{:S(2)}) copy-start(f32[24,896]{1,0:T(8,128)} %get-tuple-element.22) | copy-start | bytes 258052
  77.0 5.8 %collective-permute-start.8 = (f32[24,896]{1,0:T(8,128)S(1)}, f32[24,896]{1,0:T(8,128)S(1)}, u32[]{:S(2)}, u32[]{:S(2)}) collective-permute-start(f32[24,896]{1,0:T(8,128)S(1)} %add.47), channel_id=1, source_target_pairs={{0,16},{2,18},{4,20},{6,22},{8,24},{10,26},{12,28},{14,30},{16,0},... | collective-permute-start | bytes 258056 | tf_op jit(solution)/shard_map/ppermute | solution.py:160
  83.4 1.9 %copy-start = (f32[24,896]{1,0:T(8,128)S(1)}, f32[24,896]{1,0:T(8,128)}, u32[]{:S(2)}) copy-start(f32[24,896]{1,0:T(8,128)} %get-tuple-element.14.refs_1_) | copy-start | bytes 258052
  83.4 1.9 %copy-start.4 = (f32[24,896]{1,0:T(8,128)S(1)}, f32[24,896]{1,0:T(8,128)}, u32[]{:S(2)}) copy-start(f32[24,896]{1,0:T(8,128)} %get-tuple-element.21) | copy-start | bytes 258052
  84.0 1.4 %copy-start.2 = (f32[20,862]{1,0:T(8,128)}, f32[20,862]{1,0:T(8,128)S(1)}, u32[]{:S(2)}) copy-start(f32[20,862]{1,0:T(8,128)S(1)} %get-tuple-element.30) | copy-start | bytes 206884
  87.4 1.2 %collective-permute-start.9 = (f32[4]{0:T(128)S(1)}, f32[4]{0:T(128)S(1)}, u32[]{:S(2)}, u32[]{:S(2)}) collective-permute-start(f32[4]{0:T(128)S(1)} %pad_maximum_fusion.3), channel_id=1, source_target_pairs={{0,1},{1,0},{2,3},{3,2},{4,5},{5,4},{6,7},{7,6},{8,9},{9,8},{10,11... | collective-permute-start | bytes 56 | tf_op jit(solution)/shard_map/ppermute | solution.py:208

commit v2 on v1

--- a/solution.py
+++ b/solution.py
@@ -81,7 +81,7 @@
 
     def coarse_more(carry):
         step, low_end = carry
-        return jnp.logical_and(low_end < 0.9, step < 40)
+        return jnp.logical_and(low_end < 0.99, step < 40)
 
     def coarse(carry):
         step, low_end = carry
@@ -100,7 +100,7 @@
 
     start_gap = residual()
     start = jnp.sum(start_gap * start_gap)
-    bad = jnp.logical_not(start < 0.5)
+    bad = jnp.logical_not(start < 0.9)
 
     @pl.when(bad)
     def _():
@@ -113,7 +113,7 @@
 
     def fine_more(carry):
         step, size = carry
-        return jnp.logical_and(size > 1e-3, step < 60)
+        return jnp.logical_and(size > 5e-3, step < 60)
 
     def fine(carry):
         step, _ = carry
@@ -154,11 +154,18 @@
 
 
 def slab_sum(value, slab_count):
+    def from_peer(distance):
+        return lax.ppermute(value, "slab", [(i, i ^ distance) for i in range(slab_count)])
+
     step = 1
     while step < slab_count:
-        pairs = [(i, i ^ step) for i in range(slab_count)]
-        value = value + lax.ppermute(value, "slab", pairs)
-        step *= 2
+        if slab_count % (4 * step) == 0:
+            near, far, both = (from_peer(step * turn) for turn in (1, 2, 3))
+            value = (value + near) + (far + both)
+            step *= 4
+        else:
+            value = value + from_peer(step)
+            step *= 2
     return value
 
 

time: 91 us -> 72.7 us (0.80)
  starting transfers between devices: 33.4 us -> 17.4 us
  waiting for transfers between devices: 23.6 us -> 21.4 us
    ppermute x8 -> x12, starting transfers between devices: 32.8 us -> 16.8 us  [from_peer(): lax.ppermute(value, 'slab', [(i, i ^ distance) for i in range(slab_count)])]
    ppermute x8 -> x12, waiting for transfers between devices: 22.3 us -> 20 us  [from_peer(): lax.ppermute(value, 'slab', [(i, i ^ distance) for i in range(slab_count)])]
    add x8 -> x4, other arithmetic: 2.51 us -> 2.51 us  [slab_sum(): value = value + near + (far + both)]
  transfers between devices with their start and end apart: 10 -> 14, of which waited for: 10 -> 12; matrix products, arithmetic and copies ran while one was open for 1% -> 1% of each run, Pallas kernels for 0% -> 0%
where the time goes in v2:
time: 72.7 us; the launch traced here: 72.3 us
  waiting for transfers between devices  21.4 us (29%)
  Pallas kernels  20.4 us (28%)
  starting transfers between devices  17.4 us (24%)
  other arithmetic  6.3 us (9%)
  local copies, waits for them, and re-layouts  4.17 us (6%)
  between operations  2.68 us (4%)
    ppermute x12, waiting for transfers between devices, from_peer(): lax.ppermute(value, 'slab', [(i, i ^ distance) for i in range(slab_count)])  20 us
    ppermute x12, starting transfers between devices, from_peer(): lax.ppermute(value, 'slab', [(i, i ^ distance) for i in range(slab_count)])  16.8 us
    pallas_call x1, Pallas kernels, shards(): pl.pallas_call(first_kernel, out_shape=(flat, shape((width, rows), BF16),...  15.3 us
    pallas_call x1, Pallas kernels, shards(): pl.pallas_call(second, out_shape=(flat, flat, flat), name='second_solve')  5.15 us
    add x4, other arithmetic, slab_sum(): value = value + near + (far + both)  2.51 us
    unnamed x14, local copies, waits for them, and re-layouts  2.09 us
  transfers between devices with their start and end apart: 14, of which 12 were waited for; matrix products, arithmetic and copies ran while one was open for 1% of the time, Pallas kernels for 0%

profile of v2, /device:TPU:0, one launch (start us, length us, event | category | flops | bytes accessed | tf_op | source)
XLA Modules:
  0.0 72.3 jit_solution(865048552433090403)
XLA Ops:
  0.6 0.8 %constant_dynamic-slice_fusion.1 = (f32[20,256]{1,0:T(8,128)S(1)}, f32[20,256]{1,0:T(8,128)S(1)}) fusion(f32[40,256]{1,0:T(8,128)} %param.5, s32[]{:T(128)S(6)} %select_n.6, s32[]{:T(128)S(6)} %select_n.7), kind=kLoop, calls=%fused_computation.17 | loop fusion | bytes 81928 | tf_op jit(solution)/shard_map/dynamic_slice | solution.py:183
  2.7 0.9 %collective-permute-done = f32[61,256]{1,0:T(8,128)S(1)} collective-permute-done((f32[61,256]{1,0:T(8,128)S(1)}, f32[61,256]{1,0:T(8,128)S(1)}, u32[]{:S(2)}, u32[]{:S(2)}) %collective-permute-start) | collective-permute-done | bytes 62496 | tf_op jit(solution)/shard_map/ppermute | solution.py:186
  5.5 15.3 %first_solve.1 = (f32[24,896]{1,0:T(8,128)}, bf16[896,512]{1,0:T(8,128)(2,1)}, bf16[896,512]{1,0:T(8,128)(2,1)}, bf16[512,512]{1,0:T(8,128)(2,1)}, bf16[512,512]...) custom-call(f32[40,512]{1,0:T(8,128)} %pad_maximum_fusion.states, ...), custom_call_target="tpu_custom_call" | custom-call | tf_op jit(solution)/shard_map/first_solve/pallas_call | solution.py:193
  20.8 3.8 %collective-permute-start.3 = (f32[24,896]{1,0:T(8,128)}, f32[24,896]{1,0:T(8,128)S(1)}, u32[]{:S(2)}, u32[]{:S(2)}) collective-permute-start(f32[24,896]{1,0:T(8,128)} %get-tuple-element.14.refs_1_), channel_id=1, source_target_pairs={{0,6},{2,4},{4,2},{6,0},{8,14},{10,12},{12,10},{14,8},{16,22},{18,... | collective-permute-start | bytes 258056 | tf_op jit(solution)/shard_map/ppermute | solution.py:158
  25.2 2.7 %collective-permute-done.3 = f32[24,896]{1,0:T(8,128)S(1)} collective-permute-done((f32[24,896]{1,0:T(8,128)}, f32[24,896]{1,0:T(8,128)S(1)}, u32[]{:S(2)}, u32[]{:S(2)}) %collective-permute-start.3) | collective-permute-done | bytes 86048 | tf_op jit(solution)/shard_map/ppermute | solution.py:158
  27.8 1.6 %collective-permute-done.2 = f32[24,896]{1,0:T(8,128)S(1)} collective-permute-done((f32[24,896]{1,0:T(8,128)}, f32[24,896]{1,0:T(8,128)S(1)}, u32[]{:S(2)}, u32[]{:S(2)}) %collective-permute-start.2) | collective-permute-done | bytes 86048 | tf_op jit(solution)/shard_map/ppermute | solution.py:158
  29.7 0.9 %add_add_fusion.3 = f32[24,896]{1,0:T(8,128)S(1)} fusion(f32[24,896]{1,0:T(8,128)S(1)} %collective-permute-done.2, f32[24,896]{1,0:T(8,128)S(1)} %collective-permute-done.3, f32[24,896]{1,0:T(8,128)} %get-tuple-element.14.refs_1_, f32[24,896]{1,0:T(8,128)S(1)} %collective-permute-done.1), kind=kLoop, calls=%fused_computation.7 | loop fusion | flops 64512 | bytes 430080 | tf_op jit(solution)/shard_map/add | solution.py:164
  30.6 3.7 %collective-permute-start.6 = (f32[24,896]{1,0:T(8,128)S(1)}, f32[24,896]{1,0:T(8,128)S(1)}, u32[]{:S(2)}, u32[]{:S(2)}) collective-permute-start(f32[24,896]{1,0:T(8,128)S(1)} %add_add_fusion.3), channel_id=1, source_target_pairs={{0,24},{2,26},{4,28},{6,30},{8,16},{10,18},{12,20},{14,22},{16,8},... | collective-permute-start | bytes 258056 | tf_op jit(solution)/shard_map/ppermute | solution.py:158
  34.3 0.8 %collective-permute-start.4 = (f32[24,896]{1,0:T(8,128)S(1)}, f32[24,896]{1,0:T(8,128)S(1)}, u32[]{:S(2)}, u32[]{:S(2)}) collective-permute-start(f32[24,896]{1,0:T(8,128)S(1)} %add_add_fusion.3), channel_id=1, source_target_pairs={{0,8},{2,10},{4,12},{6,14},{8,0},{10,2},{12,4},{14,6},{16,24},{18,... | collective-permute-start | bytes 258056 | tf_op jit(solution)/shard_map/ppermute | solution.py:158
  35.1 2.9 %collective-permute-done.6 = f32[24,896]{1,0:T(8,128)S(1)} collective-permute-done((f32[24,896]{1,0:T(8,128)S(1)}, f32[24,896]{1,0:T(8,128)S(1)}, u32[]{:S(2)}, u32[]{:S(2)}) %collective-permute-start.6) | collective-permute-done | bytes 86048 | tf_op jit(solution)/shard_map/ppermute | solution.py:158
  38.0 3.5 %collective-permute-done.5 = f32[24,896]{1,0:T(8,128)S(1)} collective-permute-done((f32[24,896]{1,0:T(8,128)S(1)}, f32[24,896]{1,0:T(8,128)S(1)}, u32[]{:S(2)}, u32[]{:S(2)}) %collective-permute-start.5) | collective-permute-done | bytes 86048 | tf_op jit(solution)/shard_map/ppermute | solution.py:158
  41.6 0.7 add_add_fusion.2.refs_2_
  42.2 5.1 %second_solve.1 = (f32[24,896]{1,0:T(8,128)}, f32[24,896]{1,0:T(8,128)}, f32[24,896]{1,0:T(8,128)}) custom-call(f32[24,512]{1,0:T(8,128)} %select_maximum_fusion.targets.refs_0_, f32[24,896]{1,0:T(8,128)} %get-tuple-element.14.refs_1_, f32[24,896]{1,0:T(8,128)} %add_add_fusion.2.refs_2_, bf16[896,512]{1,0:T(8,128)(2,1)} %get-tuple-element.15.refs_3_, ...), custom_call_target="tpu_custom_call" | custom-call | tf_op jit(solution)/shard_map/second_solve/pallas_call | solution.py:204
  47.4 1.7 %collective-permute-start.9 = (f32[24,896]{1,0:T(8,128)}, f32[24,896]{1,0:T(8,128)S(1)}, u32[]{:S(2)}, u32[]{:S(2)}) collective-permute-start(f32[24,896]{1,0:T(8,128)} %get-tuple-element.23), channel_id=1, source_target_pairs={{0,6},{2,4},{4,2},{6,0},{8,14},{10,12},{12,10},{14,8},{16,22},{18,... | collective-permute-start | bytes 258056 | tf_op jit(solution)/shard_map/ppermute | solution.py:158
  49.1 1.3 %collective-permute-start.8 = (f32[24,896]{1,0:T(8,128)}, f32[24,896]{1,0:T(8,128)S(1)}, u32[]{:S(2)}, u32[]{:S(2)}) collective-permute-start(f32[24,896]{1,0:T(8,128)} %get-tuple-element.23), channel_id=1, source_target_pairs={{0,4},{2,6},{4,0},{6,2},{8,12},{10,14},{12,8},{14,10},{16,20},{18,... | collective-permute-start | bytes 258056 | tf_op jit(solution)/shard_map/ppermute | solution.py:158
  50.9 2.4 %collective-permute-done.9 = f32[24,896]{1,0:T(8,128)S(1)} collective-permute-done((f32[24,896]{1,0:T(8,128)}, f32[24,896]{1,0:T(8,128)S(1)}, u32[]{:S(2)}, u32[]{:S(2)}) %collective-permute-start.9) | collective-permute-done | bytes 86048 | tf_op jit(solution)/shard_map/ppermute | solution.py:158
  53.3 1.4 %collective-permute-done.8 = f32[24,896]{1,0:T(8,128)S(1)} collective-permute-done((f32[24,896]{1,0:T(8,128)}, f32[24,896]{1,0:T(8,128)S(1)}, u32[]{:S(2)}, u32[]{:S(2)}) %collective-permute-start.8) | collective-permute-done | bytes 86048 | tf_op jit(solution)/shard_map/ppermute | solution.py:158
  55.1 0.9 %add_add_fusion.1 = f32[24,896]{1,0:T(8,128)S(1)} fusion(f32[24,896]{1,0:T(8,128)S(1)} %collective-permute-done.8, f32[24,896]{1,0:T(8,128)S(1)} %collective-permute-done.9, f32[24,896]{1,0:T(8,128)} %get-tuple-element.23, f32[24,896]{1,0:T(8,128)S(1)} %collective-permute-done.7), kind=kLoop, calls=%fused_computation.5 | loop fusion | flops 64512 | bytes 430080 | tf_op jit(solution)/shard_map/add | solution.py:164
  56.0 2.0 %collective-permute-start.12 = (f32[24,896]{1,0:T(8,128)S(1)}, f32[24,896]{1,0:T(8,128)S(1)}, u32[]{:S(2)}, u32[]{:S(2)}) collective-permute-start(f32[24,896]{1,0:T(8,128)S(1)} %add_add_fusion.1), channel_id=1, source_target_pairs={{0,24},{2,26},{4,28},{6,30},{8,16},{10,18},{12,20},{14,22},{16,8},... | collective-permute-start | bytes 258056 | tf_op jit(solution)/shard_map/ppermute | solution.py:158
  57.9 2.5 %collective-permute-start.10 = (f32[24,896]{1,0:T(8,128)S(1)}, f32[24,896]{1,0:T(8,128)S(1)}, u32[]{:S(2)}, u32[]{:S(2)}) collective-permute-start(f32[24,896]{1,0:T(8,128)S(1)} %add_add_fusion.1), channel_id=1, source_target_pairs={{0,8},{2,10},{4,12},{6,14},{8,0},{10,2},{12,4},{14,6},{16,24},{18,... | collective-permute-start | bytes 258056 | tf_op jit(solution)/shard_map/ppermute | solution.py:158
  60.4 2.8 %collective-permute-done.12 = f32[24,896]{1,0:T(8,128)S(1)} collective-permute-done((f32[24,896]{1,0:T(8,128)S(1)}, f32[24,896]{1,0:T(8,128)S(1)}, u32[]{:S(2)}, u32[]{:S(2)}) %collective-permute-start.12) | collective-permute-done | bytes 86048 | tf_op jit(solution)/shard_map/ppermute | solution.py:158
  63.3 2.0 %collective-permute-done.11 = f32[24,896]{1,0:T(8,128)S(1)} collective-permute-done((f32[24,896]{1,0:T(8,128)S(1)}, f32[24,896]{1,0:T(8,128)S(1)}, u32[]{:S(2)}, u32[]{:S(2)}) %collective-permute-start.11) | collective-permute-done | bytes 86048 | tf_op jit(solution)/shard_map/ppermute | solution.py:158
  67.9 0.7 copy.8
  69.9 0.7 copy.7
  (38 shorter events, 8.6 us)
Async XLA Ops:
  0.6 0.9 %copy-start.3 = (f32[40,256]{1,0:T(8,128)S(1)}, f32[40,256]{1,0:T(8,128)}, u32[]{:S(2)}) copy-start(f32[40,256]{1,0:T(8,128)} %param.3) | copy-start | bytes 122884
  1.5 0.7 copy-start.5
  2.2 1.5 %collective-permute-start = (f32[61,256]{1,0:T(8,128)S(1)}, f32[61,256]{1,0:T(8,128)S(1)}, u32[]{:S(2)}, u32[]{:S(2)}) collective-permute-start(f32[61,256]{1,0:T(8,128)S(1)} %pad_maximum_fusion.1), channel_id=1, source_target_pairs={{0,1},{1,0},{2,3},{3,2},{4,5},{5,4},{6,7},{7,6},{8,9},{9,8},{10,11... | collective-permute-start | bytes 187400 | tf_op jit(solution)/shard_map/ppermute | solution.py:186
  20.8 7.1 %collective-permute-start.3 = (f32[24,896]{1,0:T(8,128)}, f32[24,896]{1,0:T(8,128)S(1)}, u32[]{:S(2)}, u32[]{:S(2)}) collective-permute-start(f32[24,896]{1,0:T(8,128)} %get-tuple-element.14.refs_1_), channel_id=1, source_target_pairs={{0,6},{2,4},{4,2},{6,0},{8,14},{10,12},{12,10},{14,8},{16,22},{18,... | collective-permute-start | bytes 258056 | tf_op jit(solution)/shard_map/ppermute | solution.py:158
  24.5 4.9 %collective-permute-start.2 = (f32[24,896]{1,0:T(8,128)}, f32[24,896]{1,0:T(8,128)S(1)}, u32[]{:S(2)}, u32[]{:S(2)}) collective-permute-start(f32[24,896]{1,0:T(8,128)} %get-tuple-element.14.refs_1_), channel_id=1, source_target_pairs={{0,4},{2,6},{4,0},{6,2},{8,12},{10,14},{12,8},{14,10},{16,20},{18,... | collective-permute-start | bytes 258056 | tf_op jit(solution)/shard_map/ppermute | solution.py:158
  25.0 4.7 %collective-permute-start.1 = (f32[24,896]{1,0:T(8,128)}, f32[24,896]{1,0:T(8,128)S(1)}, u32[]{:S(2)}, u32[]{:S(2)}) collective-permute-start(f32[24,896]{1,0:T(8,128)} %get-tuple-element.14.refs_1_), channel_id=1, source_target_pairs={{0,2},{2,0},{4,6},{6,4},{8,10},{10,8},{12,14},{14,12},{16,18},{18,... | collective-permute-start | bytes 258056 | tf_op jit(solution)/shard_map/ppermute | solution.py:158
  30.6 7.4 %collective-permute-start.6 = (f32[24,896]{1,0:T(8,128)S(1)}, f32[24,896]{1,0:T(8,128)S(1)}, u32[]{:S(2)}, u32[]{:S(2)}) collective-permute-start(f32[24,896]{1,0:T(8,128)S(1)} %add_add_fusion.3), channel_id=1, source_target_pairs={{0,24},{2,26},{4,28},{6,30},{8,16},{10,18},{12,20},{14,22},{16,8},... | collective-permute-start | bytes 258056 | tf_op jit(solution)/shard_map/ppermute | solution.py:158
  34.3 7.3 %collective-permute-start.5 = (f32[24,896]{1,0:T(8,128)S(1)}, f32[24,896]{1,0:T(8,128)S(1)}, u32[]{:S(2)}, u32[]{:S(2)}) collective-permute-start(f32[24,896]{1,0:T(8,128)S(1)} %add_add_fusion.3), channel_id=1, source_target_pairs={{0,16},{2,18},{4,20},{6,22},{8,24},{10,26},{12,28},{14,30},{16,0},... | collective-permute-start | bytes 258056 | tf_op jit(solution)/shard_map/ppermute | solution.py:158
  34.3 7.3 %collective-permute-start.4 = (f32[24,896]{1,0:T(8,128)S(1)}, f32[24,896]{1,0:T(8,128)S(1)}, u32[]{:S(2)}, u32[]{:S(2)}) collective-permute-start(f32[24,896]{1,0:T(8,128)S(1)} %add_add_fusion.3), channel_id=1, source_target_pairs={{0,8},{2,10},{4,12},{6,14},{8,0},{10,2},{12,4},{14,6},{16,24},{18,... | collective-permute-start | bytes 258056 | tf_op jit(solution)/shard_map/ppermute | solution.py:158
  47.4 5.9 %collective-permute-start.9 = (f32[24,896]{1,0:T(8,128)}, f32[24,896]{1,0:T(8,128)S(1)}, u32[]{:S(2)}, u32[]{:S(2)}) collective-permute-start(f32[24,896]{1,0:T(8,128)} %get-tuple-element.23), channel_id=1, source_target_pairs={{0,6},{2,4},{4,2},{6,0},{8,14},{10,12},{12,10},{14,8},{16,22},{18,... | collective-permute-start | bytes 258056 | tf_op jit(solution)/shard_map/ppermute | solution.py:158
  49.1 5.7 %collective-permute-start.8 = (f32[24,896]{1,0:T(8,128)}, f32[24,896]{1,0:T(8,128)S(1)}, u32[]{:S(2)}, u32[]{:S(2)}) collective-permute-start(f32[24,896]{1,0:T(8,128)} %get-tuple-element.23), channel_id=1, source_target_pairs={{0,4},{2,6},{4,0},{6,2},{8,12},{10,14},{12,8},{14,10},{16,20},{18,... | collective-permute-start | bytes 258056 | tf_op jit(solution)/shard_map/ppermute | solution.py:158
  50.4 4.7 %collective-permute-start.7 = (f32[24,896]{1,0:T(8,128)}, f32[24,896]{1,0:T(8,128)S(1)}, u32[]{:S(2)}, u32[]{:S(2)}) collective-permute-start(f32[24,896]{1,0:T(8,128)} %get-tuple-element.23), channel_id=1, source_target_pairs={{0,2},{2,0},{4,6},{6,4},{8,10},{10,8},{12,14},{14,12},{16,18},{18,... | collective-permute-start | bytes 258056 | tf_op jit(solution)/shard_map/ppermute | solution.py:158
  56.0 9.9 %copy-start.1 = (f32[24,896]{1,0:T(8,128)S(1)}, f32[24,896]{1,0:T(8,128)}, u32[]{:S(2)}) copy-start(f32[24,896]{1,0:T(8,128)} %get-tuple-element.22) | copy-start | bytes 258052
  56.0 7.3 %collective-permute-start.12 = (f32[24,896]{1,0:T(8,128)S(1)}, f32[24,896]{1,0:T(8,128)S(1)}, u32[]{:S(2)}, u32[]{:S(2)}) collective-permute-start(f32[24,896]{1,0:T(8,128)S(1)} %add_add_fusion.1), channel_id=1, source_target_pairs={{0,24},{2,26},{4,28},{6,30},{8,16},{10,18},{12,20},{14,22},{16,8},... | collective-permute-start | bytes 258056 | tf_op jit(solution)/shard_map/ppermute | solution.py:158
  57.9 7.3 %collective-permute-start.11 = (f32[24,896]{1,0:T(8,128)S(1)}, f32[24,896]{1,0:T(8,128)S(1)}, u32[]{:S(2)}, u32[]{:S(2)}) collective-permute-start(f32[24,896]{1,0:T(8,128)S(1)} %add_add_fusion.1), channel_id=1, source_target_pairs={{0,16},{2,18},{4,20},{6,22},{8,24},{10,26},{12,28},{14,30},{16,0},... | collective-permute-start | bytes 258056 | tf_op jit(solution)/shard_map/ppermute | solution.py:158
  57.9 7.3 %collective-permute-start.10 = (f32[24,896]{1,0:T(8,128)S(1)}, f32[24,896]{1,0:T(8,128)S(1)}, u32[]{:S(2)}, u32[]{:S(2)}) collective-permute-start(f32[24,896]{1,0:T(8,128)S(1)} %add_add_fusion.1), channel_id=1, source_target_pairs={{0,8},{2,10},{4,12},{6,14},{8,0},{10,2},{12,4},{14,6},{16,24},{18,... | collective-permute-start | bytes 258056 | tf_op jit(solution)/shard_map/ppermute | solution.py:158
  65.9 1.9 %copy-start = (f32[24,896]{1,0:T(8,128)S(1)}, f32[24,896]{1,0:T(8,128)}, u32[]{:S(2)}) copy-start(f32[24,896]{1,0:T(8,128)} %get-tuple-element.14.refs_1_) | copy-start | bytes 258052
  65.9 1.9 %copy-start.4 = (f32[24,896]{1,0:T(8,128)S(1)}, f32[24,896]{1,0:T(8,128)}, u32[]{:S(2)}) copy-start(f32[24,896]{1,0:T(8,128)} %get-tuple-element.21) | copy-start | bytes 258052
  66.5 1.4 %copy-start.2 = (f32[20,862]{1,0:T(8,128)}, f32[20,862]{1,0:T(8,128)S(1)}, u32[]{:S(2)}) copy-start(f32[20,862]{1,0:T(8,128)S(1)} %get-tuple-element.30) | copy-start | bytes 206884
  69.9 1.2 %collective-permute-start.13 = (f32[4]{0:T(128)S(1)}, f32[4]{0:T(128)S(1)}, u32[]{:S(2)}, u32[]{:S(2)}) collective-permute-start(f32[4]{0:T(128)S(1)} %pad_maximum_fusion.3), channel_id=1, source_target_pairs={{0,1},{1,0},{2,3},{3,2},{4,5},{5,4},{6,7},{7,6},{8,9},{9,8},{10,11... | collective-permute-start | bytes 56 | tf_op jit(solution)/shard_map/ppermute | solution.py:215

commit v3 on v2

--- a/solution.py
+++ b/solution.py
@@ -45,10 +45,16 @@
     return answer
 
 
-def first_kernel(states, inputs, targets, operator, phi_high, phi_low, kernel_high, kernel_low, inverse_high, inverse_low, phi, inverse):
-    reduced, rows = states.shape
-    x = states[...]
-    u = inputs[...]
+def first_kernel(half_rows, core, mine, other, targets, operator, phi_high, phi_low, kernel_high, kernel_low, inverse_high, inverse_low, phi, inverse):
+    reduced = 2 * half_rows
+    rows = 2 * mine.shape[1]
+    both = lambda start, stop: jnp.concatenate([mine[start:stop, :], other[start:stop, :]], 1)
+    x = both(0, reduced)
+    u = both(2 * reduced, 2 * reduced + 1)
+    aims = both(reduced, 2 * reduced)
+    picked = jnp.where(core[0] == 0, aims[:half_rows], aims[half_rows:])
+    targets[...] = jnp.zeros(targets.shape, F32)
+    targets[0:half_rows, :] = picked
     width = phi.shape[0]
     offset = 0
     phi[0:reduced, :] = x
@@ -143,7 +149,7 @@
     answer = refined(right_side, kernel[0], kernel[1], (inverse_high[...], inverse_low[...]), 1)
     second = shifted + product3(split(answer), phi, NT)
     mean_out[...] = mean
-    next_operator[...] = second
+    next_operator[...] = second[: next_operator.shape[0], : next_operator.shape[1]]
     primal = jnp.sum(duals * duals)
     moved = second - mean
     spread = jnp.sum(moved * moved)
@@ -151,6 +157,25 @@
     column = lax.broadcasted_iota(jnp.int32, first.shape, 1)
     extra = jnp.where(column == 0, primal, jnp.where(column == 1, spread, 0.0))
     summand[...] = jnp.where(row == half_rows, extra, second + duals)
+
+
+def closing_kernel(slabs, half_rows, operator, mean, second, total, consensus, duals, sums):
+    height, width = consensus.shape
+    before = mean[0:height, 0:width]
+    latest = total[0:height, 0:width] / slabs
+    consensus[...] = latest
+    duals[...] = operator[0:height, 0:width] - before + second[...] - latest
+    first_dual = slabs * penalty * penalty * jnp.sum(jnp.square(before))
+    moved = slabs * jnp.sum(jnp.square(latest - before))
+    scalars = total[half_rows : half_rows + 1, 0:128]
+    lane = lax.broadcasted_iota(jnp.int32, scalars.shape, 1)
+    first_primal = jnp.sum(jnp.where(lane == 0, scalars, 0.0))
+    second_primal = jnp.sum(jnp.where(lane == 1, scalars, 0.0)) - moved
+    row = lax.broadcasted_iota(jnp.int32, sums.shape, 0)
+    column = lax.broadcasted_iota(jnp.int32, sums.shape, 1)
+    primal = jnp.where(column == 0, first_primal, second_primal)
+    dual = jnp.where(column == 0, first_dual, penalty * penalty * moved)
+    sums[...] = jnp.where(row == 0, primal, dual)
 
 
 def slab_sum(value, slab_count):
@@ -180,42 +205,44 @@
     height = (half_rows // 8 + 1) * 8
     core = lax.axis_index("feat")
     swap = [(i, (i + 1) % feat_count) for i in range(feat_count)]
-    own = lax.dynamic_slice_in_dim(targets, core * half_rows, half_rows, 0)
-    theirs = lax.dynamic_slice_in_dim(targets, (1 - core) * half_rows, half_rows, 0)
-    packed = jnp.concatenate([states, theirs, inputs[None]], 0)
+    packed = jnp.concatenate([states, targets, inputs[None]], 0)
     other = lax.ppermute(packed, "feat", swap)
-    all_states = jnp.concatenate([states, other[:reduced]], 1)
-    all_inputs = jnp.concatenate([inputs[None], other[reduced + half_rows :]], 1)
-    picked = jnp.concatenate([own, other[reduced : reduced + half_rows]], 1)
-    picked = jnp.pad(picked, ((0, height - half_rows), (0, 0)))
     shape = jax.ShapeDtypeStruct
     flat = shape((height, width), F32)
-    operator, *kept = pl.pallas_call(
-        first_kernel,
-        out_shape=(flat, shape((width, rows), BF16), shape((width, rows), BF16)) + (shape((rows, rows), BF16),) * 4,
+    block = shape((half_rows, features), F32)
+    whole = pl.BlockSpec(memory_space=pltpu.VMEM)
+
+    def first(*refs):
+        first_kernel(half_rows, *refs)
+
+    picked, operator, *kept = pl.pallas_call(
+        first,
+        out_shape=(shape((height, rows), F32), flat, shape((width, rows), BF16), shape((width, rows), BF16))
+        + (shape((rows, rows), BF16),) * 4,
+        in_specs=[pl.BlockSpec(memory_space=pltpu.SMEM), whole, whole],
         scratch_shapes=[pltpu.VMEM((width, rows), F32), pltpu.VMEM((rows, rows), F32)],
         name="first_solve",
-    )(all_states, all_inputs, picked)
+    )(core.reshape(1).astype(jnp.int32), packed, other)
     total = slab_sum(operator, slab_count)
 
     def second(*refs):
         second_kernel(slab_count, features, half_rows, *refs)
 
-    mean, second_operator, summand = pl.pallas_call(second, out_shape=(flat, flat, flat), name="second_solve")(
+    mean, second_operator, summand = pl.pallas_call(second, out_shape=(flat, block, flat), name="second_solve")(
         picked, operator, total, *kept
     )
     total = slab_sum(summand, slab_count)
-    keep = lambda value: value[:half_rows, :features]
-    consensus = keep(total) / slab_count
-    before = keep(mean)
-    duals = keep(operator) - before + keep(second_operator) - consensus
-    first_dual = slab_count * penalty * penalty * jnp.sum(jnp.square(before))
-    moved = slab_count * jnp.sum(jnp.square(consensus - before))
-    sums = jnp.stack([total[half_rows, 0], total[half_rows, 1] - moved, first_dual, penalty * penalty * moved])
+
+    def closing(*refs):
+        closing_kernel(slab_count, half_rows, *refs)
+
+    consensus, duals, sums = pl.pallas_call(closing, out_shape=(block, block, shape((2, 2), F32)), name="closing")(
+        operator, mean, second_operator, total
+    )
     sums = sums + lax.ppermute(sums, "feat", swap)
-    history = jnp.maximum(sums, 0.0).reshape(2, 2)
+    history = jnp.maximum(sums, 0.0)
     residual_history = jnp.sqrt(history / (slab_count * reduced * features))
-    return (keep(second_operator)[None], duals[None], consensus, residual_history)
+    return (second_operator[None], duals[None], consensus, residual_history)
 
 
 def solution(mesh):

time: 72.7 us -> 71.2 us (0.979)
  between operations: 2.68 us -> 0.67 us
  other arithmetic: 6.3 us -> 4.54 us
  Pallas kernels: 20.4 us -> 21.7 us
  starting transfers between devices: 17.4 us -> 18.2 us
    unnamed x14 -> x12, local copies, waits for them, and re-layouts: 2.09 us -> 4.28 us
    pallas_call x2 -> x3, Pallas kernels: 20.4 us -> 21.7 us  [the longest x1 14.8 us: shards(): pl.pallas_call(first, out_shape=(shape((height, rows), F32), flat, shape(...]
    concatenate x4 -> x1, other arithmetic: 1.86 us -> 0.81 us  [shards(): packed = jnp.concatenate([states, targets, inputs[None]], 0)]
    dynamic_slice x1 -> x0, local copies, waits for them, and re-layouts: 0.83 us -> none  [shards(): own = lax.dynamic_slice_in_dim(targets, core * half_rows, half_rows, 0)]
    ppermute x12, starting transfers between devices: 16.8 us -> 17.6 us  [from_peer(): lax.ppermute(value, 'slab', [(i, i ^ distance) for i in range(slab_count)])]
where the time goes in v3:
time: 71.2 us; the launch traced here: 70.9 us
  Pallas kernels  21.7 us (30%)
  waiting for transfers between devices  21.5 us (30%)
  starting transfers between devices  18.2 us (26%)
  other arithmetic  4.54 us (6%)
  local copies, waits for them, and re-layouts  4.28 us (6%)
    ppermute x12, waiting for transfers between devices, from_peer(): lax.ppermute(value, 'slab', [(i, i ^ distance) for i in range(slab_count)])  19.4 us
    ppermute x12, starting transfers between devices, from_peer(): lax.ppermute(value, 'slab', [(i, i ^ distance) for i in range(slab_count)])  17.6 us
    pallas_call x1, Pallas kernels, shards(): pl.pallas_call(first, out_shape=(shape((height, rows), F32), flat, shape(...  14.8 us
    pallas_call x1, Pallas kernels, shards(): pl.pallas_call(second, out_shape=(flat, block, flat), name='second_solve')  5.15 us
    unnamed x12, local copies, waits for them, and re-layouts  4.28 us
    add x4, other arithmetic, slab_sum(): value = value + near + (far + both)  3.16 us
    pallas_call x1, Pallas kernels, shards(): pl.pallas_call(closing, out_shape=(block, block, shape((2, 2), F32)), nam...  1.74 us
  transfers between devices with their start and end apart: 14, of which 12 were waited for; matrix products, arithmetic and copies ran while one was open for 1% of the time, Pallas kernels for 0%

profile of v3, /device:TPU:0, one launch (start us, length us, event | category | flops | bytes accessed | tf_op | source)
XLA Modules:
  0.0 70.9 jit_solution(13004577854779612842)
XLA Ops:
  1.3 0.8 %pad_maximum_fusion.refs_1_ = f32[81,256]{1,0:T(8,128)S(1)} fusion(f32[1,256]{1,0:T(1,128)S(1)} %bitcast.6, f32[40,256]{1,0:T(8,128)} %param.5, f32[40,256]{1,0:T(8,128)} %param.3), kind=kLoop, calls=%fused_computation | loop fusion | flops 41472 | bytes 165888 | tf_op jit(solution)/shard_map/concatenate | solution.py:208
  2.7 0.9 %collective-permute-done.refs_2_ = f32[81,256]{1,0:T(8,128)S(1)} collective-permute-done((f32[81,256]{1,0:T(8,128)S(1)}, f32[81,256]{1,0:T(8,128)S(1)}, u32[]{:S(2)}, u32[]{:S(2)}) %collective-permute-start) | collective-permute-done | bytes 82976 | tf_op jit(solution)/shard_map/ppermute | solution.py:209
  4.2 14.8 %first_solve.1 = (f32[24,512]{1,0:T(8,128)}, f32[24,896]{1,0:T(8,128)}, bf16[896,512]{1,0:T(8,128)(2,1)}, bf16[896,512]{1,0:T(8,128)(2,1)}, bf16[512,512]{1,0:T(...) custom-call(s32[1]{0:T(128)} %bitcast.refs_0_, f32[81,256]{1,0:T(8,128)} %copy-done, ...), custom_call_target="tpu_custom_call" | custom-call | tf_op jit(solution)/shard_map/first_solve/pallas_call | solution.py:218
  19.1 4.6 %collective-permute-start.3 = (f32[24,896]{1,0:T(8,128)}, f32[24,896]{1,0:T(8,128)S(1)}, u32[]{:S(2)}, u32[]{:S(2)}) collective-permute-start(f32[24,896]{1,0:T(8,128)} %get-tuple-element.19.refs_1_.refs_0_), channel_id=1, source_target_pairs={{0,6},{2,4},{4,2},{6,0},{8,14},{10,12},{12,10},{14,8},{16,22},{18,... | collective-permute-start | bytes 258056 | tf_op jit(solution)/shard_map/ppermute | solution.py:183
  24.3 2.6 %collective-permute-done.3 = f32[24,896]{1,0:T(8,128)S(1)} collective-permute-done((f32[24,896]{1,0:T(8,128)}, f32[24,896]{1,0:T(8,128)S(1)}, u32[]{:S(2)}, u32[]{:S(2)}) %collective-permute-start.3) | collective-permute-done | bytes 86048 | tf_op jit(solution)/shard_map/ppermute | solution.py:183
  26.9 1.6 %collective-permute-done.2 = f32[24,896]{1,0:T(8,128)S(1)} collective-permute-done((f32[24,896]{1,0:T(8,128)}, f32[24,896]{1,0:T(8,128)S(1)}, u32[]{:S(2)}, u32[]{:S(2)}) %collective-permute-start.2) | collective-permute-done | bytes 86048 | tf_op jit(solution)/shard_map/ppermute | solution.py:183
  28.8 0.9 %add_add_fusion.3 = f32[24,896]{1,0:T(8,128)S(1)} fusion(f32[24,896]{1,0:T(8,128)S(1)} %collective-permute-done.2, f32[24,896]{1,0:T(8,128)S(1)} %collective-permute-done.3, f32[24,896]{1,0:T(8,128)} %get-tuple-element.19.refs_1_.refs_0_, f32[24,896]{1,0:T(8,128)S(1)} %collective-permute-done.1), kind=kLoop, calls=%fused_computation.4 | loop fusion | flops 64512 | bytes 430080 | tf_op jit(solution)/shard_map/add | solution.py:189
  29.8 3.6 %collective-permute-start.6 = (f32[24,896]{1,0:T(8,128)S(1)}, f32[24,896]{1,0:T(8,128)S(1)}, u32[]{:S(2)}, u32[]{:S(2)}) collective-permute-start(f32[24,896]{1,0:T(8,128)S(1)} %add_add_fusion.3), channel_id=1, source_target_pairs={{0,24},{2,26},{4,28},{6,30},{8,16},{10,18},{12,20},{14,22},{16,8},... | collective-permute-start | bytes 258056 | tf_op jit(solution)/shard_map/ppermute | solution.py:183
  33.3 0.9 %collective-permute-start.4 = (f32[24,896]{1,0:T(8,128)S(1)}, f32[24,896]{1,0:T(8,128)S(1)}, u32[]{:S(2)}, u32[]{:S(2)}) collective-permute-start(f32[24,896]{1,0:T(8,128)S(1)} %add_add_fusion.3), channel_id=1, source_target_pairs={{0,8},{2,10},{4,12},{6,14},{8,0},{10,2},{12,4},{14,6},{16,24},{18,... | collective-permute-start | bytes 258056 | tf_op jit(solution)/shard_map/ppermute | solution.py:183
  34.2 3.0 %collective-permute-done.6 = f32[24,896]{1,0:T(8,128)S(1)} collective-permute-done((f32[24,896]{1,0:T(8,128)S(1)}, f32[24,896]{1,0:T(8,128)S(1)}, u32[]{:S(2)}, u32[]{:S(2)}) %collective-permute-start.6) | collective-permute-done | bytes 86048 | tf_op jit(solution)/shard_map/ppermute | solution.py:183
  37.2 3.5 %collective-permute-done.5 = f32[24,896]{1,0:T(8,128)S(1)} collective-permute-done((f32[24,896]{1,0:T(8,128)S(1)}, f32[24,896]{1,0:T(8,128)S(1)}, u32[]{:S(2)}, u32[]{:S(2)}) %collective-permute-start.5) | collective-permute-done | bytes 86048 | tf_op jit(solution)/shard_map/ppermute | solution.py:183
  41.3 5.2 %second_solve.1 = (f32[24,896]{1,0:T(8,128)}, f32[20,862]{1,0:T(8,128)}, f32[24,896]{1,0:T(8,128)}) custom-call(f32[24,512]{1,0:T(8,128)} %get-tuple-element.18.refs_0_, f32[24,896]{1,0:T(8,128)} %get-tuple-element.19.refs_1_.refs_0_, f32[24,896]{1,0:T(8,128)} %add_add_fusion.2.refs_2_, bf16[896,512]{1,0:T(8,128)(2,1)} %get-tuple-element.20.refs_3_, ...), custom_call_target="tpu_custom_call" | custom-call | tf_op jit(solution)/shard_map/second_solve/pallas_call | solution.py:231
  46.5 1.6 %collective-permute-start.9 = (f32[24,896]{1,0:T(8,128)}, f32[24,896]{1,0:T(8,128)S(1)}, u32[]{:S(2)}, u32[]{:S(2)}) collective-permute-start(f32[24,896]{1,0:T(8,128)} %get-tuple-element.28), channel_id=1, source_target_pairs={{0,6},{2,4},{4,2},{6,0},{8,14},{10,12},{12,10},{14,8},{16,22},{18,... | collective-permute-start | bytes 258056 | tf_op jit(solution)/shard_map/ppermute | solution.py:183
  48.7 1.2 %collective-permute-start.7 = (f32[24,896]{1,0:T(8,128)}, f32[24,896]{1,0:T(8,128)S(1)}, u32[]{:S(2)}, u32[]{:S(2)}) collective-permute-start(f32[24,896]{1,0:T(8,128)} %get-tuple-element.28), channel_id=1, source_target_pairs={{0,2},{2,0},{4,6},{6,4},{8,10},{10,8},{12,14},{14,12},{16,18},{18,... | collective-permute-start | bytes 258056 | tf_op jit(solution)/shard_map/ppermute | solution.py:183
  50.0 3.0 %collective-permute-done.9 = f32[24,896]{1,0:T(8,128)S(1)} collective-permute-done((f32[24,896]{1,0:T(8,128)}, f32[24,896]{1,0:T(8,128)S(1)}, u32[]{:S(2)}, u32[]{:S(2)}) %collective-permute-start.9) | collective-permute-done | bytes 86048 | tf_op jit(solution)/shard_map/ppermute | solution.py:183
  53.7 0.9 %add_add_fusion.1 = f32[24,896]{1,0:T(8,128)S(1)} fusion(f32[24,896]{1,0:T(8,128)S(1)} %collective-permute-done.8, f32[24,896]{1,0:T(8,128)S(1)} %collective-permute-done.9, f32[24,896]{1,0:T(8,128)} %get-tuple-element.28, f32[24,896]{1,0:T(8,128)S(1)} %collective-permute-done.7), kind=kLoop, calls=%fused_computation.2 | loop fusion | flops 64512 | bytes 430080 | tf_op jit(solution)/shard_map/add | solution.py:189
  54.6 2.5 %collective-permute-start.12 = (f32[24,896]{1,0:T(8,128)S(1)}, f32[24,896]{1,0:T(8,128)S(1)}, u32[]{:S(2)}, u32[]{:S(2)}) collective-permute-start(f32[24,896]{1,0:T(8,128)S(1)} %add_add_fusion.1), channel_id=1, source_target_pairs={{0,24},{2,26},{4,28},{6,30},{8,16},{10,18},{12,20},{14,22},{16,8},... | collective-permute-start | bytes 258056 | tf_op jit(solution)/shard_map/ppermute | solution.py:183
  57.0 2.0 %collective-permute-start.10 = (f32[24,896]{1,0:T(8,128)S(1)}, f32[24,896]{1,0:T(8,128)S(1)}, u32[]{:S(2)}, u32[]{:S(2)}) collective-permute-start(f32[24,896]{1,0:T(8,128)S(1)} %add_add_fusion.1), channel_id=1, source_target_pairs={{0,8},{2,10},{4,12},{6,14},{8,0},{10,2},{12,4},{14,6},{16,24},{18,... | collective-permute-start | bytes 258056 | tf_op jit(solution)/shard_map/ppermute | solution.py:183
  59.0 0.7 copy.7
  59.7 2.0 %collective-permute-done.12 = f32[24,896]{1,0:T(8,128)S(1)} collective-permute-done((f32[24,896]{1,0:T(8,128)S(1)}, f32[24,896]{1,0:T(8,128)S(1)}, u32[]{:S(2)}, u32[]{:S(2)}) %collective-permute-start.12) | collective-permute-done | bytes 86048 | tf_op jit(solution)/shard_map/ppermute | solution.py:183
  61.7 2.7 %collective-permute-done.11 = f32[24,896]{1,0:T(8,128)S(1)} collective-permute-done((f32[24,896]{1,0:T(8,128)S(1)}, f32[24,896]{1,0:T(8,128)S(1)}, u32[]{:S(2)}, u32[]{:S(2)}) %collective-permute-start.11) | collective-permute-done | bytes 86048 | tf_op jit(solution)/shard_map/ppermute | solution.py:183
  65.1 1.7 %closing.1 = (f32[20,862]{1,0:T(8,128)}, f32[20,862]{1,0:T(8,128)}, f32[2,2]{1,0:T(2,128)}) custom-call(f32[24,896]{1,0:T(8,128)} %get-tuple-element.19.refs_1_.refs_0_, f32[24,896]{1,0:T(8,128)} %get-tuple-element.27.refs_1_, f32[20,862]{1,0:T(8,128)} %get-tuple-element.26.refs_2_, f32[24,896]{1,0:T(8,128)} %add_add_fusion.refs_3_), custom_call_target="tpu_custom_call" | custom-call | tf_op jit(solution)/shard_map/closing/pallas_call | solution.py:239
  66.8 1.6 %copy.8 = f32[1,20,862]{2,0,1:T(1,128)} copy(f32[1,20,862]{2,1,0:T(8,128)} %bitcast.5) | data formatting | bytes 137920
  69.1 1.2 %collective-permute-done.13 = f32[2,2]{1,0:T(2,128)S(1)} collective-permute-done((f32[2,2]{1,0:T(2,128)S(1)}, f32[2,2]{1,0:T(2,128)S(1)}, u32[]{:S(2)}, u32[]{:S(2)}) %collective-permute-start.13) | collective-permute-done | bytes 48 | tf_op jit(solution)/shard_map/ppermute | solution.py:242
  (25 shorter events, 6.7 us)
Async XLA Ops:
  0.6 0.7 copy-start.3
  2.1 1.5 %copy-start = (f32[81,256]{1,0:T(8,128)}, f32[81,256]{1,0:T(8,128)S(1)}, u32[]{:S(2)}) copy-start(f32[81,256]{1,0:T(8,128)S(1)} %pad_maximum_fusion.refs_1_) | copy-start | bytes 248836
  2.1 1.5 %collective-permute-start = (f32[81,256]{1,0:T(8,128)S(1)}, f32[81,256]{1,0:T(8,128)S(1)}, u32[]{:S(2)}, u32[]{:S(2)}) collective-permute-start(f32[81,256]{1,0:T(8,128)S(1)} %pad_maximum_fusion.refs_1_), channel_id=1, source_target_pairs={{0,1},{1,0},{2,3},{3,2},{4,5},{5,4},{6,7},{7,6},{8,9},{9,8},{10,11... | collective-permute-start | bytes 248840 | tf_op jit(solution)/shard_map/ppermute | solution.py:209
  3.6 0.6 copy-start.2
  19.1 7.9 %collective-permute-start.3 = (f32[24,896]{1,0:T(8,128)}, f32[24,896]{1,0:T(8,128)S(1)}, u32[]{:S(2)}, u32[]{:S(2)}) collective-permute-start(f32[24,896]{1,0:T(8,128)} %get-tuple-element.19.refs_1_.refs_0_), channel_id=1, source_target_pairs={{0,6},{2,4},{4,2},{6,0},{8,14},{10,12},{12,10},{14,8},{16,22},{18,... | collective-permute-start | bytes 258056 | tf_op jit(solution)/shard_map/ppermute | solution.py:183
  23.6 4.9 %collective-permute-start.2 = (f32[24,896]{1,0:T(8,128)}, f32[24,896]{1,0:T(8,128)S(1)}, u32[]{:S(2)}, u32[]{:S(2)}) collective-permute-start(f32[24,896]{1,0:T(8,128)} %get-tuple-element.19.refs_1_.refs_0_), channel_id=1, source_target_pairs={{0,4},{2,6},{4,0},{6,2},{8,12},{10,14},{12,8},{14,10},{16,20},{18,... | collective-permute-start | bytes 258056 | tf_op jit(solution)/shard_map/ppermute | solution.py:183
  24.1 4.7 %collective-permute-start.1 = (f32[24,896]{1,0:T(8,128)}, f32[24,896]{1,0:T(8,128)S(1)}, u32[]{:S(2)}, u32[]{:S(2)}) collective-permute-start(f32[24,896]{1,0:T(8,128)} %get-tuple-element.19.refs_1_.refs_0_), channel_id=1, source_target_pairs={{0,2},{2,0},{4,6},{6,4},{8,10},{10,8},{12,14},{14,12},{16,18},{18,... | collective-permute-start | bytes 258056 | tf_op jit(solution)/shard_map/ppermute | solution.py:183
  29.8 7.4 %collective-permute-start.6 = (f32[24,896]{1,0:T(8,128)S(1)}, f32[24,896]{1,0:T(8,128)S(1)}, u32[]{:S(2)}, u32[]{:S(2)}) collective-permute-start(f32[24,896]{1,0:T(8,128)S(1)} %add_add_fusion.3), channel_id=1, source_target_pairs={{0,24},{2,26},{4,28},{6,30},{8,16},{10,18},{12,20},{14,22},{16,8},... | collective-permute-start | bytes 258056 | tf_op jit(solution)/shard_map/ppermute | solution.py:183
  33.3 7.3 %collective-permute-start.5 = (f32[24,896]{1,0:T(8,128)S(1)}, f32[24,896]{1,0:T(8,128)S(1)}, u32[]{:S(2)}, u32[]{:S(2)}) collective-permute-start(f32[24,896]{1,0:T(8,128)S(1)} %add_add_fusion.3), channel_id=1, source_target_pairs={{0,16},{2,18},{4,20},{6,22},{8,24},{10,26},{12,28},{14,30},{16,0},... | collective-permute-start | bytes 258056 | tf_op jit(solution)/shard_map/ppermute | solution.py:183
  33.3 7.3 %collective-permute-start.4 = (f32[24,896]{1,0:T(8,128)S(1)}, f32[24,896]{1,0:T(8,128)S(1)}, u32[]{:S(2)}, u32[]{:S(2)}) collective-permute-start(f32[24,896]{1,0:T(8,128)S(1)} %add_add_fusion.3), channel_id=1, source_target_pairs={{0,8},{2,10},{4,12},{6,14},{8,0},{10,2},{12,4},{14,6},{16,24},{18,... | collective-permute-start | bytes 258056 | tf_op jit(solution)/shard_map/ppermute | solution.py:183
  46.5 12.6 %copy-start.1 = (f32[20,862]{1,0:T(8,128)S(1)}, f32[20,862]{1,0:T(8,128)}, u32[]{:S(2)}) copy-start(f32[20,862]{1,0:T(8,128)} %get-tuple-element.26.refs_2_) | copy-start | bytes 206884
  46.5 6.5 %collective-permute-start.9 = (f32[24,896]{1,0:T(8,128)}, f32[24,896]{1,0:T(8,128)S(1)}, u32[]{:S(2)}, u32[]{:S(2)}) collective-permute-start(f32[24,896]{1,0:T(8,128)} %get-tuple-element.28), channel_id=1, source_target_pairs={{0,6},{2,4},{4,2},{6,0},{8,14},{10,12},{12,10},{14,8},{16,22},{18,... | collective-permute-start | bytes 258056 | tf_op jit(solution)/shard_map/ppermute | solution.py:183
  48.1 5.2 %collective-permute-start.8 = (f32[24,896]{1,0:T(8,128)}, f32[24,896]{1,0:T(8,128)S(1)}, u32[]{:S(2)}, u32[]{:S(2)}) collective-permute-start(f32[24,896]{1,0:T(8,128)} %get-tuple-element.28), channel_id=1, source_target_pairs={{0,4},{2,6},{4,0},{6,2},{8,12},{10,14},{12,8},{14,10},{16,20},{18,... | collective-permute-start | bytes 258056 | tf_op jit(solution)/shard_map/ppermute | solution.py:183
  48.7 4.9 %collective-permute-start.7 = (f32[24,896]{1,0:T(8,128)}, f32[24,896]{1,0:T(8,128)S(1)}, u32[]{:S(2)}, u32[]{:S(2)}) collective-permute-start(f32[24,896]{1,0:T(8,128)} %get-tuple-element.28), channel_id=1, source_target_pairs={{0,2},{2,0},{4,6},{6,4},{8,10},{10,8},{12,14},{14,12},{16,18},{18,... | collective-permute-start | bytes 258056 | tf_op jit(solution)/shard_map/ppermute | solution.py:183
  54.6 7.1 %collective-permute-start.12 = (f32[24,896]{1,0:T(8,128)S(1)}, f32[24,896]{1,0:T(8,128)S(1)}, u32[]{:S(2)}, u32[]{:S(2)}) collective-permute-start(f32[24,896]{1,0:T(8,128)S(1)} %add_add_fusion.1), channel_id=1, source_target_pairs={{0,24},{2,26},{4,28},{6,30},{8,16},{10,18},{12,20},{14,22},{16,8},... | collective-permute-start | bytes 258056 | tf_op jit(solution)/shard_map/ppermute | solution.py:183
  57.0 7.4 %collective-permute-start.11 = (f32[24,896]{1,0:T(8,128)S(1)}, f32[24,896]{1,0:T(8,128)S(1)}, u32[]{:S(2)}, u32[]{:S(2)}) collective-permute-start(f32[24,896]{1,0:T(8,128)S(1)} %add_add_fusion.1), channel_id=1, source_target_pairs={{0,16},{2,18},{4,20},{6,22},{8,24},{10,26},{12,28},{14,30},{16,0},... | collective-permute-start | bytes 258056 | tf_op jit(solution)/shard_map/ppermute | solution.py:183
  57.0 7.4 %collective-permute-start.10 = (f32[24,896]{1,0:T(8,128)S(1)}, f32[24,896]{1,0:T(8,128)S(1)}, u32[]{:S(2)}, u32[]{:S(2)}) collective-permute-start(f32[24,896]{1,0:T(8,128)S(1)} %add_add_fusion.1), channel_id=1, source_target_pairs={{0,8},{2,10},{4,12},{6,14},{8,0},{10,2},{12,4},{14,6},{16,24},{18,... | collective-permute-start | bytes 258056 | tf_op jit(solution)/shard_map/ppermute | solution.py:183
  68.4 0.7 copy-start.4
  69.1 1.2 %collective-permute-start.13 = (f32[2,2]{1,0:T(2,128)S(1)}, f32[2,2]{1,0:T(2,128)S(1)}, u32[]{:S(2)}, u32[]{:S(2)}) collective-permute-start(f32[2,2]{1,0:T(2,128)S(1)} %copy-done.4), channel_id=1, source_target_pairs={{0,1},{1,0},{2,3},{3,2},{4,5},{5,4},{6,7},{7,6},{8,9},{9,8},{10,11... | collective-permute-start | bytes 56 | tf_op jit(solution)/shard_map/ppermute | solution.py:242
